TPU v7x, 32 devices: a whole 2x2x4 slice. The times are simulated.
32 devices in a mesh: shot: 8 (over z, y), grid: 4 (over x, core).
Axes of the slice: x: 2, y: 2, z: 4, core: 2. Of those that a mesh axis runs over, the one named last changes fastest.
Arguments:
- residuals: bfloat16 [2048, 4, 512], P('shot', None, 'grid'), may hold values from -6 to 6
- encoding: bfloat16 [8, 2048], P(None, 'shot'), may hold values from -0.1875 to 0.1875
- receiver_cells: int32 [3, 512], replicated, may hold values from 0 to 127, as said below
- velocity_term: float32 [64, 128, 256], P('grid'), may hold values from 0.02 to 0.18
- field_before: float32 [8, 64, 128, 256], P('shot', 'grid'), may hold values from -6 to 6
- field_start: float32 [8, 64, 128, 256], P('shot', 'grid'), may hold values from -6 to 6
Outputs:
- field_last: float32 [8, 64, 128, 256], P('shot', 'grid')
- field_end: float32 [8, 64, 128, 256], P('shot', 'grid')
Inputs may be any that keep to these rules, and one draw needn't show every extreme that they name: `receiver_cells`: row 0 holds first-dimension cells below 64, row 1 second-dimension cells below 128, row 2 third-dimension cells below 8.
All inputs are finite; a program needn't handle non-finite values.
Results may differ from a plain program's by a relative error of at most 0.0003.
Values sent between devices are 32-bit elements; how exact they have to be, the bound alone decides.
No kernel may reach another device: no remote copies, remote signals or barrier semaphores. Data moves between devices by JAX's collectives and lax.ppermute only.
A program may use at most 128 MiB of HBM per device.

v0:
```python
import jax
import jax.numpy as jnp
from jax import lax
from jax.sharding import PartitionSpec as P

coeffs = (-205.0 / 72.0, 8.0 / 5.0, -1.0 / 5.0, 8.0 / 315.0, -1.0 / 560.0)


def extended_2(shard, sides, width):
    for axis, dim in sides:
        size, length = (lax.axis_size(axis), shard.shape[dim])
        up = [(i, (i + 1) % size) for i in range(size - 1)]
        down = [(j, i) for i, j in up]
        last = lax.slice_in_dim(shard, length - width, length, axis=dim)
        initial = lax.slice_in_dim(shard, 0, width, axis=dim)
        before = lax.ppermute(last, axis, up)
        after = lax.ppermute(initial, axis, down)
        shard = jnp.concatenate([before, shard, after], axis=dim)
    return shard


def laplace(extended):
    width = extended.shape[0] - 8
    center = extended[4 : 4 + width]
    padded = jnp.pad(center, ((0, 0), (4, 4), (4, 4)))
    rows = center.shape[1]
    depth = center.shape[2]
    total = 3.0 * coeffs[0] * center
    for shift in range(1, 5):
        along_x = extended[4 + shift : 4 + shift + width] + extended[4 - shift : 4 - shift + width]
        along_y = (
            padded[:, 4 + shift : 4 + shift + rows, 4 : 4 + depth]
            + padded[:, 4 - shift : 4 - shift + rows, 4 : 4 + depth]
        )
        along_z = (
            padded[:, 4 : 4 + rows, 4 + shift : 4 + shift + depth]
            + padded[:, 4 : 4 + rows, 4 - shift : 4 - shift + depth]
        )
        total = total + coeffs[shift] * (along_x + along_y + along_z)
    return total


def inject(field, start_x, cells, values):
    width, rows, depth = field.shape
    local_x = cells[0] - start_x
    inside = (local_x >= 0) & (local_x < width)
    flat = (local_x * rows + cells[1]) * depth + cells[2]
    flat = jnp.where(inside, flat, width * rows * depth)
    return field.reshape(-1).at[flat].add(values, mode="drop").reshape(field.shape)


def local(residuals, encoding, receiver_cells, velocity_term, field_before, field_start):
    shot_rows, samples, local_receivers = residuals.shape
    flat_data = residuals.reshape(shot_rows, samples * local_receivers)
    own_traces = lax.psum_scatter(
        jnp.dot(encoding, flat_data, preferred_element_type=jnp.float32),
        "shot",
        scatter_dimension=0,
        tiled=True,
    )
    own_traces = own_traces.reshape(samples, local_receivers)
    traces = lax.all_gather(own_traces, "grid", axis=1, tiled=True)
    width = velocity_term.shape[0]
    start_x = lax.axis_index("grid") * width
    previous = field_before[0]
    current = field_start[0]
    for step in range(samples):
        extended = extended_2(current, (("grid", 0),), 4)
        advanced = 2.0 * current - previous + velocity_term * laplace(extended)
        advanced = inject(advanced, start_x, receiver_cells, traces[samples - 1 - step])
        previous, current = (current, advanced)
    return (previous[None], current[None])


def solution(mesh):
    return jax.shard_map(
        local,
        mesh=mesh,
        in_specs=(
            P("shot", None, "grid"),
            P(None, "shot"),
            P(),
            P("grid", None, None),
            P("shot", "grid", None, None),
            P("shot", "grid", None, None),
        ),
        out_specs=(P("shot", "grid", None, None), P("shot", "grid", None, None)),
        check_vma=False,
    )
```

profile of v0, /device:TPU:1, one launch (start us, length us, event | category | flops | bytes accessed | tf_op | source)
XLA Modules:
  0.0 166.0 jit_solution(5070472384700058914)
XLA Ops:
  0.7 2.4 %slice_bitcast_fusion.1 = (f32[4,128,256]{2,1,0:T(8,128)}, f32[4,128,256]{2,1,0:T(8,128)}) fusion(f32[1,16,128,256]{3,2,1,0:T(8,128)} %param.11), kind=kLoop, calls=%fused_computation.210 | loop fusion | bytes 2097152 | tf_op jit(solution)/shard_map/slice | solution.py:15
  3.1 1.9 %collective-permute-start = (f32[4,128,256]{2,1,0:T(8,128)}, f32[4,128,256]{2,1,0:T(8,128)S(1)}, u32[]{:S(2)}, u32[]{:S(2)}) collective-permute-start(f32[4,128,256]{2,1,0:T(8,128)} %get-tuple-element.14), channel_id=1, source_target_pairs={{1,0},{2,1},{3,2},{5,4},{6,5},{7,6},{9,8},{10,9},{11,10},{13,12},{... | collective-permute-start | bytes 1572872 | tf_op jit(solution)/shard_map/ppermute | solution.py:17
  5.0 4.5 %collective-permute-start.1 = (f32[4,128,256]{2,1,0:T(8,128)}, f32[4,128,256]{2,1,0:T(8,128)S(1)}, u32[]{:S(2)}, u32[]{:S(2)}) collective-permute-start(f32[4,128,256]{2,1,0:T(8,128)} %get-tuple-element.15), channel_id=1, source_target_pairs={{0,1},{1,2},{2,3},{4,5},{5,6},{6,7},{8,9},{9,10},{10,11},{12,13},{... | collective-permute-start | bytes 1572872 | tf_op jit(solution)/shard_map/ppermute | solution.py:16
  9.7 30.4 %all-reduce.4 = f32[8,512]{1,0:T(8,128)S(1)} all-reduce(f32[8,512]{1,0:T(8,128)S(1)} %fusion.114), channel_id=2, replica_groups=mesh['shot'=8,'grid'=4] {'shot'}, use_global_device_ids=true, to_apply=%region_0.0.clone | all-reduce | flops 4096 | bytes 32768
  41.2 11.5 %all_gather.3 = f32[4,512]{1,0:T(4,128)S(1)} all-gather(f32[4,128]{1,0:T(4,128)S(1)} %bitcast.50), channel_id=1, replica_groups=mesh['shot'=8,'grid'=4] {'grid'}, dimensions={1}, use_global_device_ids=true | all-gather | bytes 10240 | tf_op jit(solution)/shard_map/all_gather | solution.py:62
  52.7 30.5 %fusion.8 = f32[16,128,256]{2,1,0:T(8,128)S(1)} fusion(f32[16,128,256]{2,1,0:T(8,128)S(1)} %copy-done.5, f32[16,128,256]{2,1,0:T(8,128)} %bitcast.36, f32[4,128,256]{2,1,0:T(8,128)S(1)} %collective-permute-done.1, f32[4,128,256]{2,1,0:T(8,128)S(1)} %collective-permute-done, f32[1,16,128,256]{3,2,1,0:T(8,128)} %param.10), kind=kLoop, calls=%fused_computation.88 | loop fusion | flops 21495808 | bytes 9437184 | tf_op jit(solution)/shard_map/add | solution.py:69
  84.3 4.1 %scatter_fusion = f32[524288]{0:T(1024)S(1)} fusion(f32[524288]{0:T(1024)S(1)} %bitcast.33, s32[512]{0:T(512)S(1)} %bitcast.42, f32[512]{0:T(512)S(1)} %bitcast.49), kind=kCustom, calls=%fused_computation | custom fusion | flops 512 | bytes 8192 | tf_op jit(solution)/shard_map/scatter-add | solution.py:49
  89.7 3.2 %collective-permute-start.3 = (f32[4,128,256]{2,1,0:T(8,128)}, f32[4,128,256]{2,1,0:T(8,128)}, u32[]{:S(2)}, u32[]{:S(2)}) collective-permute-start(f32[4,128,256]{2,1,0:T(8,128)} %slice.482), channel_id=1, source_target_pairs={{0,1},{1,2},{2,3},{4,5},{5,6},{6,7},{8,9},{9,10},{10,11},{12,13},{... | collective-permute-start | bytes 1572872 | tf_op jit(solution)/shard_map/ppermute | solution.py:16
  93.1 2.0 %collective-permute-start.2 = (f32[4,128,256]{2,1,0:T(8,128)S(1)}, f32[4,128,256]{2,1,0:T(8,128)S(1)}, u32[]{:S(2)}, u32[]{:S(2)}) collective-permute-start(f32[4,128,256]{2,1,0:T(8,128)S(1)} %slice.479), channel_id=1, source_target_pairs={{1,0},{2,1},{3,2},{5,4},{6,5},{7,6},{9,8},{10,9},{11,10},{13,12},{... | collective-permute-start | bytes 1572872 | tf_op jit(solution)/shard_map/ppermute | solution.py:17
  96.9 2.4 %collective-permute-done.3 = f32[4,128,256]{2,1,0:T(8,128)} collective-permute-done((f32[4,128,256]{2,1,0:T(8,128)}, f32[4,128,256]{2,1,0:T(8,128)}, u32[]{:S(2)}, u32[]{:S(2)}) %collective-permute-start.3) | collective-permute-done | bytes 524320 | tf_op jit(solution)/shard_map/ppermute | solution.py:16
  100.9 2.7 %collective-permute-done.2 = f32[4,128,256]{2,1,0:T(8,128)S(1)} collective-permute-done((f32[4,128,256]{2,1,0:T(8,128)S(1)}, f32[4,128,256]{2,1,0:T(8,128)S(1)}, u32[]{:S(2)}, u32[]{:S(2)}) %collective-permute-start.2) | collective-permute-done | bytes 524320 | tf_op jit(solution)/shard_map/ppermute | solution.py:17
  103.6 4.8 %fusion.44 = f32[16,128,256]{2,1,0:T(8,128)S(1)} fusion(f32[16,128,256]{2,1,0:T(8,128)S(1)} %copy-done.6, f32[16,128,256]{2,1,0:T(8,128)S(1)} %reshape.159, f32[20,128,256]{2,1,0:T(8,128)S(1)} %get-tuple-element.13, f32[20,128,256]{2,1,0:T(8,128)S(1)} %constant_dynamic-update-slice_fusion, f32[1,16,128,256]{3,2,1,0:T(8,128)S(1)} %copy-done.12), kind=kLoop, calls=%fused_computation.124 | loop fusion | flops 17301504 | bytes 25165824 | tf_op jit(solution)/shard_map/add | solution.py:69
  109.5 4.1 %scatter_fusion.1 = f32[524288]{0:T(1024)S(1)} fusion(f32[524288]{0:T(1024)S(1)} %bitcast.34, s32[512]{0:T(512)S(1)} %bitcast.43, f32[512]{0:T(512)S(1)} %bitcast.48), kind=kCustom, calls=%fused_computation.1 | custom fusion | flops 512 | bytes 8192 | tf_op jit(solution)/shard_map/scatter-add | solution.py:49
  114.9 3.3 %collective-permute-start.5 = (f32[4,128,256]{2,1,0:T(8,128)}, f32[4,128,256]{2,1,0:T(8,128)}, u32[]{:S(2)}, u32[]{:S(2)}) collective-permute-start(f32[4,128,256]{2,1,0:T(8,128)} %slice.511), channel_id=1, source_target_pairs={{0,1},{1,2},{2,3},{4,5},{5,6},{6,7},{8,9},{9,10},{10,11},{12,13},{... | collective-permute-start | bytes 1572872 | tf_op jit(solution)/shard_map/ppermute | solution.py:16
  118.4 2.1 %collective-permute-start.4 = (f32[4,128,256]{2,1,0:T(8,128)S(1)}, f32[4,128,256]{2,1,0:T(8,128)S(1)}, u32[]{:S(2)}, u32[]{:S(2)}) collective-permute-start(f32[4,128,256]{2,1,0:T(8,128)S(1)} %slice.508), channel_id=1, source_target_pairs={{1,0},{2,1},{3,2},{5,4},{6,5},{7,6},{9,8},{10,9},{11,10},{13,12},{... | collective-permute-start | bytes 1572872 | tf_op jit(solution)/shard_map/ppermute | solution.py:17
  122.4 2.2 %collective-permute-done.5 = f32[4,128,256]{2,1,0:T(8,128)} collective-permute-done((f32[4,128,256]{2,1,0:T(8,128)}, f32[4,128,256]{2,1,0:T(8,128)}, u32[]{:S(2)}, u32[]{:S(2)}) %collective-permute-start.5) | collective-permute-done | bytes 524320 | tf_op jit(solution)/shard_map/ppermute | solution.py:16
  126.2 2.7 %collective-permute-done.4 = f32[4,128,256]{2,1,0:T(8,128)S(1)} collective-permute-done((f32[4,128,256]{2,1,0:T(8,128)S(1)}, f32[4,128,256]{2,1,0:T(8,128)S(1)}, u32[]{:S(2)}, u32[]{:S(2)}) %collective-permute-start.4) | collective-permute-done | bytes 524320 | tf_op jit(solution)/shard_map/ppermute | solution.py:17
  129.0 4.8 %fusion.70 = f32[16,128,256]{2,1,0:T(8,128)S(1)} fusion(f32[16,128,256]{2,1,0:T(8,128)S(1)} %copy-done.7, f32[16,128,256]{2,1,0:T(8,128)S(1)} %reshape.161, f32[20,128,256]{2,1,0:T(8,128)S(1)} %get-tuple-element.9, f32[20,128,256]{2,1,0:T(8,128)S(1)} %constant_dynamic-update-slice_fusion.4, f32[16,128,256]{2,1,0:T(8,128)S(1)} %copy-done.4), kind=kLoop, calls=%fused_computation.150 | loop fusion | flops 17301504 | bytes 25165824 | tf_op jit(solution)/shard_map/add | solution.py:69
  134.8 4.1 %scatter_fusion.2 = f32[524288]{0:T(1024)S(1)} fusion(f32[524288]{0:T(1024)S(1)} %bitcast.32, s32[512]{0:T(512)S(1)} %bitcast.44, f32[512]{0:T(512)S(1)} %bitcast.47), kind=kCustom, calls=%fused_computation.2 | custom fusion | flops 512 | bytes 8192 | tf_op jit(solution)/shard_map/scatter-add | solution.py:49
  140.0 3.3 %collective-permute-start.7 = (f32[4,128,256]{2,1,0:T(8,128)}, f32[4,128,256]{2,1,0:T(8,128)}, u32[]{:S(2)}, u32[]{:S(2)}) collective-permute-start(f32[4,128,256]{2,1,0:T(8,128)} %slice.540), channel_id=1, source_target_pairs={{0,1},{1,2},{2,3},{4,5},{5,6},{6,7},{8,9},{9,10},{10,11},{12,13},{... | collective-permute-start | bytes 1572872 | tf_op jit(solution)/shard_map/ppermute | solution.py:16
  143.5 1.9 %collective-permute-start.6 = (f32[4,128,256]{2,1,0:T(8,128)S(1)}, f32[4,128,256]{2,1,0:T(8,128)S(1)}, u32[]{:S(2)}, u32[]{:S(2)}) collective-permute-start(f32[4,128,256]{2,1,0:T(8,128)S(1)} %slice.537), channel_id=1, source_target_pairs={{1,0},{2,1},{3,2},{5,4},{6,5},{7,6},{9,8},{10,9},{11,10},{13,12},{... | collective-permute-start | bytes 1572872 | tf_op jit(solution)/shard_map/ppermute | solution.py:17
  150.9 2.2 %constant_dynamic-update-slice_fusion.9 = (f32[20,128,256]{2,1,0:T(8,128)S(1)}, f32[20,128,256]{2,1,0:T(8,128)S(1)}) fusion(f32[16,128,256]{2,1,0:T(8,128)} %reshape.163, f32[20,128,256]{2,1,0:T(8,128)S(1)} %constant_dynamic-update-slice_fusion.11), kind=kLoop, calls=%fused_computation.223 | loop fusion | bytes 6291456
  154.3 4.9 %fusion.96 = f32[16,128,256]{2,1,0:T(8,128)S(1)} fusion(f32[16,128,256]{2,1,0:T(8,128)S(1)} %copy-done.8, f32[16,128,256]{2,1,0:T(8,128)S(1)} %copy-done.11, f32[20,128,256]{2,1,0:T(8,128)S(1)} %get-tuple-element.5, f32[20,128,256]{2,1,0:T(8,128)S(1)} %constant_dynamic-update-slice_fusion.8, f32[16,128,256]{2,1,0:T(8,128)S(1)} %copy-done.2), kind=kLoop, calls=%fused_computation.176 | loop fusion | flops 17301504 | bytes 25165824 | tf_op jit(solution)/shard_map/add | solution.py:69
  160.3 4.1 %scatter_fusion.3 = f32[524288]{0:T(1024)S(1)} fusion(f32[524288]{0:T(1024)S(1)} %bitcast.35, s32[512]{0:T(512)S(1)} %bitcast.45, f32[512]{0:T(512)S(1)} %bitcast.46), kind=kCustom, calls=%fused_computation.3 | custom fusion | flops 512 | bytes 8192 | tf_op jit(solution)/shard_map/scatter-add | solution.py:49
  (67 shorter events, 24.9 us)
Async XLA Ops:
  0.6 8.9 %copy-start = (bf16[8,256]{1,0:T(8,128)(2,1)S(1)}, bf16[8,256]{1,0:T(8,128)(2,1)}, u32[]{:S(2)}) copy-start(bf16[8,256]{1,0:T(8,128)(2,1)} %param.7) | copy-start | bytes 12292
  0.6 39.4 %copy-start.15 = (u32[32]{0:T(128)S(1)}, u32[32]{0:T(128)}, u32[]{:S(2)}) copy-start(u32[32]{0:T(128)} %constant.43) | copy-start | bytes 388
  0.7 8.9 %copy-start.13 = (bf16[256,4,128]{2,1,0:T(4,128)(2,1)S(1)}, bf16[256,4,128]{2,1,0:T(4,128)(2,1)}, u32[]{:S(2)}) copy-start(bf16[256,4,128]{2,1,0:T(4,128)(2,1)} %param.6) | copy-start | bytes 786436
  0.7 52.0 %copy-start.14 = (s32[3,512]{1,0:T(4,128)S(1)}, s32[3,512]{1,0:T(4,128)}, u32[]{:S(2)}) copy-start(s32[3,512]{1,0:T(4,128)} %param.8) | copy-start | bytes 18436
  0.7 52.0 %copy-start.5 = (f32[16,128,256]{2,1,0:T(8,128)S(1)}, f32[16,128,256]{2,1,0:T(8,128)}, u32[]{:S(2)}) copy-start(f32[16,128,256]{2,1,0:T(8,128)} %param.9) | copy-start | bytes 6291460
  3.1 49.6 %collective-permute-start = (f32[4,128,256]{2,1,0:T(8,128)}, f32[4,128,256]{2,1,0:T(8,128)S(1)}, u32[]{:S(2)}, u32[]{:S(2)}) collective-permute-start(f32[4,128,256]{2,1,0:T(8,128)} %get-tuple-element.14), channel_id=1, source_target_pairs={{1,0},{2,1},{3,2},{5,4},{6,5},{7,6},{9,8},{10,9},{11,10},{13,12},{... | collective-permute-start | bytes 1572872 | tf_op jit(solution)/shard_map/ppermute | solution.py:17
  5.0 47.7 %collective-permute-start.1 = (f32[4,128,256]{2,1,0:T(8,128)}, f32[4,128,256]{2,1,0:T(8,128)S(1)}, u32[]{:S(2)}, u32[]{:S(2)}) collective-permute-start(f32[4,128,256]{2,1,0:T(8,128)} %get-tuple-element.15), channel_id=1, source_target_pairs={{0,1},{1,2},{2,3},{4,5},{5,6},{6,7},{8,9},{9,10},{10,11},{12,13},{... | collective-permute-start | bytes 1572872 | tf_op jit(solution)/shard_map/ppermute | solution.py:16
  88.4 4.6 %copy-start.9 = (f32[524288]{0:T(1024)}, f32[524288]{0:T(1024)S(1)}, u32[]{:S(2)}) copy-start(f32[524288]{0:T(1024)S(1)} %scatter_fusion) | copy-start | bytes 6291460
  89.7 9.6 %collective-permute-start.3 = (f32[4,128,256]{2,1,0:T(8,128)}, f32[4,128,256]{2,1,0:T(8,128)}, u32[]{:S(2)}, u32[]{:S(2)}) collective-permute-start(f32[4,128,256]{2,1,0:T(8,128)} %slice.482), channel_id=1, source_target_pairs={{0,1},{1,2},{2,3},{4,5},{5,6},{6,7},{8,9},{9,10},{10,11},{12,13},{... | collective-permute-start | bytes 1572872 | tf_op jit(solution)/shard_map/ppermute | solution.py:16
  93.1 10.5 %collective-permute-start.2 = (f32[4,128,256]{2,1,0:T(8,128)S(1)}, f32[4,128,256]{2,1,0:T(8,128)S(1)}, u32[]{:S(2)}, u32[]{:S(2)}) collective-permute-start(f32[4,128,256]{2,1,0:T(8,128)S(1)} %slice.479), channel_id=1, source_target_pairs={{1,0},{2,1},{3,2},{5,4},{6,5},{7,6},{9,8},{10,9},{11,10},{13,12},{... | collective-permute-start | bytes 1572872 | tf_op jit(solution)/shard_map/ppermute | solution.py:17
  96.9 6.7 %copy-start.3 = (f32[16,128,256]{2,1,0:T(8,128)}, f32[16,128,256]{2,1,0:T(8,128)S(1)}, u32[]{:S(2)}) copy-start(f32[16,128,256]{2,1,0:T(8,128)S(1)} %reshape.159) | copy-start | bytes 6291460
  100.4 3.2 %copy-start.6 = (f32[16,128,256]{2,1,0:T(8,128)S(1)}, f32[16,128,256]{2,1,0:T(8,128)}, u32[]{:S(2)}) copy-start(f32[16,128,256]{2,1,0:T(8,128)} %param.9) | copy-start | bytes 6291460
  100.4 3.2 %copy-start.12 = (f32[1,16,128,256]{3,2,1,0:T(8,128)S(1)}, f32[1,16,128,256]{3,2,1,0:T(8,128)}, u32[]{:S(2)}) copy-start(f32[1,16,128,256]{3,2,1,0:T(8,128)} %param.11) | copy-start | bytes 6291460
  113.6 4.8 %copy-start.10 = (f32[524288]{0:T(1024)}, f32[524288]{0:T(1024)S(1)}, u32[]{:S(2)}) copy-start(f32[524288]{0:T(1024)S(1)} %scatter_fusion.1) | copy-start | bytes 6291460
  114.9 9.8 %collective-permute-start.5 = (f32[4,128,256]{2,1,0:T(8,128)}, f32[4,128,256]{2,1,0:T(8,128)}, u32[]{:S(2)}, u32[]{:S(2)}) collective-permute-start(f32[4,128,256]{2,1,0:T(8,128)} %slice.511), channel_id=1, source_target_pairs={{0,1},{1,2},{2,3},{4,5},{5,6},{6,7},{8,9},{9,10},{10,11},{12,13},{... | collective-permute-start | bytes 1572872 | tf_op jit(solution)/shard_map/ppermute | solution.py:16
  118.4 10.5 %collective-permute-start.4 = (f32[4,128,256]{2,1,0:T(8,128)S(1)}, f32[4,128,256]{2,1,0:T(8,128)S(1)}, u32[]{:S(2)}, u32[]{:S(2)}) collective-permute-start(f32[4,128,256]{2,1,0:T(8,128)S(1)} %slice.508), channel_id=1, source_target_pairs={{1,0},{2,1},{3,2},{5,4},{6,5},{7,6},{9,8},{10,9},{11,10},{13,12},{... | collective-permute-start | bytes 1572872 | tf_op jit(solution)/shard_map/ppermute | solution.py:17
  122.4 6.5 %copy-start.1 = (f32[16,128,256]{2,1,0:T(8,128)}, f32[16,128,256]{2,1,0:T(8,128)S(1)}, u32[]{:S(2)}) copy-start(f32[16,128,256]{2,1,0:T(8,128)S(1)} %reshape.161) | copy-start | bytes 6291460
  125.7 3.2 %copy-start.4 = (f32[16,128,256]{2,1,0:T(8,128)S(1)}, f32[16,128,256]{2,1,0:T(8,128)}, u32[]{:S(2)}) copy-start(f32[16,128,256]{2,1,0:T(8,128)} %copy-done.3) | copy-start | bytes 6291460
  125.7 3.2 %copy-start.7 = (f32[16,128,256]{2,1,0:T(8,128)S(1)}, f32[16,128,256]{2,1,0:T(8,128)}, u32[]{:S(2)}) copy-start(f32[16,128,256]{2,1,0:T(8,128)} %param.9) | copy-start | bytes 6291460
  140.0 9.8 %collective-permute-start.7 = (f32[4,128,256]{2,1,0:T(8,128)}, f32[4,128,256]{2,1,0:T(8,128)}, u32[]{:S(2)}, u32[]{:S(2)}) collective-permute-start(f32[4,128,256]{2,1,0:T(8,128)} %slice.540), channel_id=1, source_target_pairs={{0,1},{1,2},{2,3},{4,5},{5,6},{6,7},{8,9},{9,10},{10,11},{12,13},{... | collective-permute-start | bytes 1572872 | tf_op jit(solution)/shard_map/ppermute | solution.py:16
  143.5 10.5 %collective-permute-start.6 = (f32[4,128,256]{2,1,0:T(8,128)S(1)}, f32[4,128,256]{2,1,0:T(8,128)S(1)}, u32[]{:S(2)}, u32[]{:S(2)}) collective-permute-start(f32[4,128,256]{2,1,0:T(8,128)S(1)} %slice.537), channel_id=1, source_target_pairs={{1,0},{2,1},{3,2},{5,4},{6,5},{7,6},{9,8},{10,9},{11,10},{13,12},{... | collective-permute-start | bytes 1572872 | tf_op jit(solution)/shard_map/ppermute | solution.py:17
  150.8 3.2 %copy-start.2 = (f32[16,128,256]{2,1,0:T(8,128)S(1)}, f32[16,128,256]{2,1,0:T(8,128)}, u32[]{:S(2)}) copy-start(f32[16,128,256]{2,1,0:T(8,128)} %copy-done.1) | copy-start | bytes 6291460
  150.8 3.2 %copy-start.8 = (f32[16,128,256]{2,1,0:T(8,128)S(1)}, f32[16,128,256]{2,1,0:T(8,128)}, u32[]{:S(2)}) copy-start(f32[16,128,256]{2,1,0:T(8,128)} %param.9) | copy-start | bytes 6291460
  150.8 3.5 %copy-start.11 = (f32[16,128,256]{2,1,0:T(8,128)S(1)}, f32[16,128,256]{2,1,0:T(8,128)}, u32[]{:S(2)}) copy-start(f32[16,128,256]{2,1,0:T(8,128)} %reshape.163) | copy-start | bytes 6291460
where the time goes:
time: 167 us; the launch traced here: 166 us
  other arithmetic  61.3 us (37%)
  blocking collectives  41.8 us (25%)
  local copies, waits for them, and re-layouts  27.3 us (16%)
  starting transfers between devices  22.2 us (13%)
  waiting for transfers between devices  12 us (7%)
    add x4, other arithmetic, local(): advanced = 2.0 * current - previous + velocity_term * laplace(extended)  44.9 us
    unnamed x1, blocking collectives  30.4 us
    scatter-add x4, other arithmetic, inject(): field.reshape(-1).at[flat].add(values, mode='drop').reshape(field.shape)  16.4 us
    ppermute x4, starting transfers between devices, extended_2(): before = lax.ppermute(last, axis, up)  14.3 us
    unnamed x44, local copies, waits for them, and re-layouts  12.2 us
    all_gather x1, blocking collectives, local(): traces = lax.all_gather(own_traces, 'grid', axis=1, tiled=True)  11.5 us
    ppermute x4, starting transfers between devices, extended_2(): after = lax.ppermute(initial, axis, down)  7.89 us
    ppermute x4, waiting for transfers between devices, extended_2(): after = lax.ppermute(initial, axis, down)  6.23 us
  transfers between devices with their start and end apart: 8, of which 6 were waited for; matrix products, arithmetic and copies ran while one was open for 9% of the time, Pallas kernels for 0%

commit v1 on v0

v1 whole, which is shorter than its diff:
```python
import functools

import jax
import jax.numpy as jnp
import numpy as np
from jax import lax
from jax.experimental import pallas as pl
from jax.experimental.pallas import tpu as pltpu
from jax.sharding import PartitionSpec as P

scale = 5040.0
weights = (-14350.0, 8064.0, -1008.0, 128.0, -9.0)
coeffs = tuple(w / scale for w in weights)
reach = 4
near = 8
lanes = 128

VMEM = pl.BlockSpec(memory_space=pltpu.VMEM)
HBM = pl.BlockSpec(memory_space=pltpu.HBM)


def band(size):
    offset = np.abs(np.arange(size)[:, None] - np.arange(size)[None, :])
    table = np.zeros((size, size), np.float32)
    for j in range(1, reach + 1):
        table[offset == j] = weights[j]
    return table


def odd_device():
    return lax.rem(lax.axis_index("grid"), 2)


def pick(odd, if_odd, if_even):
    return odd * if_odd + (1 - odd) * if_even


def part_of(parts, u):
    first, middle, last = parts
    if u < reach:
        return first.at[u]
    if u < reach + middle.shape[0]:
        return middle.at[u - reach]
    return last.at[u - reach - middle.shape[0]]


def raw_of(ref, odd, u):
    width = ref.shape[-3]
    at = pick(odd, u, width - 1 - u)
    return ref.at[0, at] if len(ref.shape) == 4 else ref.at[at]


def step_kernel(raw_cur, raw_prev, injected, final, width, *refs):
    refs = list(refs)
    take = lambda n: tuple(refs.pop(0) for _ in range(n))
    cur_parts = take(1 if raw_cur else 3)
    prev_parts = take(1 if raw_prev else 3) if not (raw_cur and False) else ()
    (vel, halo, zband, yband) = take(4)
    inject = take(1)[0] if injected else None
    outs = take(2 if final else 3)
    sums = take(1)[0]
    odd = odd_device()
    rows, depth = vel.shape[1], vel.shape[2]

    def cur(u):
        if u < 0:
            k = -1 - u
            return halo.at[pick(odd, reach - 1 - k, k)] if raw_cur else halo.at[k]
        return raw_of(cur_parts[0], odd, u) if raw_cur else part_of(cur_parts, u)

    def prev(u):
        return raw_of(prev_parts[0], odd, u) if raw_prev else part_of(prev_parts, u)

    if final:
        whole, last = outs
        ready, sem = take(2)

        def out(u):
            return ready.at[u] if u < width - reach else last.at[u - width + reach]

        def copy(u):
            return pltpu.make_async_copy(ready.at[u], raw_of(whole, odd, u), sem.at[u])
    else:

        def out(u):
            return part_of(outs, u)

    chunk = 32
    for u in range(width):
        field = cur(u)[...]
        high = field.astype(jnp.bfloat16)
        low = (field - high.astype(jnp.float32)).astype(jnp.bfloat16)
        along_z = jnp.dot(jnp.concatenate([high, low], axis=1), zband[...], preferred_element_type=jnp.float32)
        along_y = jnp.dot(yband[...], jnp.concatenate([high, low], axis=0), preferred_element_type=jnp.float32)
        sums[u] = along_y + along_z
        for at in range(0, rows, chunk):
            part = pl.ds(at, min(chunk, rows - at))
            here = cur(u)[part, :]
            total = sums[u, part, :] * (1.0 / scale) + (3.0 * coeffs[0]) * here
            for j in range(1, reach + 1):
                pair = cur(u - j)[part, :]
                if u + j < width:
                    pair = pair + cur(u + j)[part, :]
                total = total + coeffs[j] * pair
            result = (here + here) - prev(u)[part, :] + raw_of(vel, odd, u)[part, :] * total
            out(u)[part, :] = result
            if injected:
                out(u)[part, :lanes] = result[:, :lanes] + inject[u, part, :]
        if final and 1 <= u <= width - reach:
            copy(u - 1).start()
    if final:
        for u in range(width - reach):
            copy(u).wait()


def edge_kernel(raw, injected, final, width, *refs):
    refs = list(refs)
    take = lambda n: tuple(refs.pop(0) for _ in range(n))
    (partial, vel, halo) = take(3)
    inject = take(1)[0] if injected else None
    if final:
        take(1)
    out = take(1)[0]
    if final:
        result, sem = take(2)
    else:
        result = out
    odd = odd_device()
    rows = vel.shape[1]
    chunk = 32

    def copy(i):
        return pltpu.make_async_copy(result.at[i], raw_of(out, odd, width - reach + i), sem.at[i])

    for i in range(reach):
        u = width - reach + i
        for at in range(0, rows, chunk):
            part = pl.ds(at, min(chunk, rows - at))
            total = None
            small = None
            for j in range(reach - i, reach + 1):
                h = i + j - reach
                index = pick(odd, h, reach - 1 - h) if raw else reach - 1 - h
                term = coeffs[j] * halo[index, part, :]
                total = term if total is None else total + term
                if injected:
                    term = coeffs[j] * inject[reach - 1 - h, part, :]
                    small = term if small is None else small + term
            factor = raw_of(vel, odd, u)[part, :]
            value = partial[i, part, :] + factor * total
            result[i, part, :] = value
            if injected:
                result[i, part, :lanes] = value[:, :lanes] + factor[:, :lanes] * small
        if final and i >= 1:
            copy(i - 1).start()
    if final:
        copy(reach - 1).start()
        for i in range(reach):
            copy(i).wait()


def inject_kernel(shots, samples, width, sent, cells, first, middle, last, halo, o_first, o_middle, o_last, o_halo, o_edge, *o_steps):
    odd = odd_device()
    groups = sent.shape[0] // shots
    own = sent.shape[1] // samples
    rows = first.shape[1]
    start = lax.axis_index("grid") * width
    traces = sent[0:groups, :]
    for s in range(1, shots):
        traces = traces + sent[s * groups : (s + 1) * groups, :]
    margin = lanes // near
    totals = [None] * samples
    per = max(1, 512 // own)
    for g0 in range(0, groups, per):
        gs = range(g0, min(groups, g0 + per))
        span = slice(g0 * own, (gs[-1] + 1) * own)
        x = cells[0:1, span] - start
        u = pick(odd, x, width - 1 - x)
        y = cells[1:2, span]
        z = cells[2:3, span]
        count = y.shape[1]
        at_row = jnp.where(lax.broadcasted_iota(jnp.int32, (rows, count), 0) == y, 1.0, 0.0).astype(jnp.bfloat16)
        at_row = jnp.concatenate([at_row, at_row], axis=1)
        for n in range(samples):
            t = samples - 1 - n
            value = jnp.concatenate([traces[g : g + 1, t * own : (t + 1) * own] for g in gs], axis=1)
            size = (width + 2 * reach) * near if n == 0 else width * near
            low_u = -reach if n == 0 else 0
            inside = (u >= low_u) & (u < low_u + size // near)
            cell = jnp.where(inside, (u - low_u) * near + z, -1)
            weighted = jnp.where(lax.broadcasted_iota(jnp.int32, (size, count), 0) == cell, value, 0.0)
            high = weighted.astype(jnp.bfloat16)
            rest = weighted - high.astype(jnp.float32)
            mid = rest.astype(jnp.bfloat16)
            both = jnp.concatenate([high, mid], axis=1)
            out = lax.dot_general(at_row, both, (((1,), (1,)), ((), ())), preferred_element_type=jnp.float32)
            totals[n] = out if totals[n] is None else totals[n] + out
    inside = lax.broadcasted_iota(jnp.int32, (rows, lanes), 1) < near

    def spread(n, k):
        base = k * near // lanes * lanes
        tile = totals[n][:, base : base + lanes]
        if tile.shape[1] < lanes:
            tile = jnp.concatenate([tile, jnp.zeros((rows, lanes - tile.shape[1]), jnp.float32)], axis=1)
        shift = k * near - base
        moved = pltpu.roll(tile, lanes - shift, 1) if shift else tile
        return jnp.where(inside, moved, 0.0)

    for k in range(width + 2 * reach):
        u = k - reach
        extra = spread(0, k)
        if u >= width:
            o_edge[width + reach - 1 - u] = extra
            continue
        if u < 0:
            source, target = halo.at[-1 - u], o_halo.at[-1 - u]
        else:
            source = part_of((first, middle, last), u)
            target = part_of((o_first, o_middle, o_last), u)
        target[:, lanes:] = source[:, lanes:]
        target[:, :lanes] = source[:, :lanes] + extra
    for n in range(1, samples):
        for u in range(width):
            o_steps[n - 1][u] = spread(n, u)


def gather_kernel(width, first, middle, last, whole, sem):
    odd = odd_device()
    copies = [pltpu.make_async_copy(part_of((first, middle, last), u), raw_of(whole, odd, u), sem.at[u]) for u in range(width)]
    for copy in copies:
        copy.start()
    for copy in copies:
        copy.wait()


def params(mib):
    return pltpu.CompilerParams(vmem_limit_bytes=mib * 1024 * 1024)


def local(residuals, encoding, receiver_cells, velocity_term, field_before, field_start):
    shot_rows, samples, own = residuals.shape
    width, rows, depth = velocity_term.shape
    groups, shots = lax.axis_size("grid"), lax.axis_size("shot")
    odd = lax.axis_index("grid") % 2
    f32 = jnp.float32
    shape = lambda *s: jax.ShapeDtypeStruct(s, f32)
    core_pairs = [(i, i ^ 1) for i in range(groups) if i ^ 1 < groups]
    chip_pairs = [(i, j) for i in range(groups) for j in [((i + 1) ^ 1) - 1] if 0 <= j < groups]

    zband = jnp.asarray(np.concatenate([band(depth)] * 2, axis=0), jnp.bfloat16)
    yband = jnp.asarray(np.concatenate([band(rows)] * 2, axis=1), jnp.bfloat16)

    to_chip = lax.dynamic_slice_in_dim(field_start[0], odd * (width - reach), reach, 0)
    to_core = lax.dynamic_slice_in_dim(field_start[0], (1 - odd) * (width - reach), reach, 0)
    chip_halo = lax.ppermute(to_chip, "grid", chip_pairs)
    core_halo = lax.ppermute(to_core, "grid", core_pairs)

    partial = jnp.dot(encoding, residuals.reshape(shot_rows, samples * own), preferred_element_type=f32)
    sent = jnp.broadcast_to(partial[:, None], (shots, groups, samples * own)).reshape(shots * groups, samples * own)
    sent = lax.all_to_all(sent, ("shot", "grid"), 0, 0, tiled=True)

    middle = width - 2 * reach
    previous, current = (field_before,), (field_start,)
    injections = [None] * samples
    edge_injection = None
    for n in range(samples):
        final = n == samples - 1
        raw_cur, raw_prev = len(current) == 1, len(previous) == 1
        inject = injections[n]
        layer_parts = [shape(reach, rows, depth), shape(middle, rows, depth), shape(reach, rows, depth)]
        results = pl.pallas_call(
            functools.partial(step_kernel, raw_cur, raw_prev, inject is not None, final, width),
            out_shape=[shape(1, width, rows, depth), layer_parts[2]] if final else layer_parts,
            in_specs=[VMEM] * (len(current) + len(previous) + 4 + (inject is not None)),
            out_specs=[HBM, VMEM] if final else [VMEM] * 3,
            scratch_shapes=[pltpu.VMEM((width, rows, depth), f32)]
            + ([pltpu.VMEM((width - reach, rows, depth), f32), pltpu.SemaphoreType.DMA((width - reach,))] if final else []),
            compiler_params=params(24),
            cost_estimate=pl.CostEstimate(flops=900_000_000, bytes_accessed=8_000_000, transcendentals=0),
            name=f"step{n}",
        )(*current, *previous, velocity_term, core_halo, zband, yband, *(() if inject is None else (inject,)))
        partial_edge = results[-1]
        extra = () if edge_injection is None else (edge_injection,)
        if final:
            (end,) = pl.pallas_call(
                functools.partial(edge_kernel, raw_cur, bool(extra), True, width),
                out_shape=[shape(1, width, rows, depth)],
                in_specs=[VMEM] * (3 + len(extra)) + [HBM],
                out_specs=[HBM],
                scratch_shapes=[pltpu.VMEM((reach, rows, depth), f32), pltpu.SemaphoreType.DMA((reach,))],
                input_output_aliases={3 + len(extra): 0},
                compiler_params=params(16),
                name=f"edge{n}",
            )(partial_edge, velocity_term, chip_halo, *extra, results[0])
            (last,) = pl.pallas_call(
                functools.partial(gather_kernel, width),
                out_shape=[shape(1, width, rows, depth)],
                in_specs=[VMEM] * 3,
                out_specs=[HBM],
                scratch_shapes=[pltpu.SemaphoreType.DMA((width,))],
                compiler_params=params(16),
                name="gather",
            )(*current)
            return last, end
        (edge,) = pl.pallas_call(
            functools.partial(edge_kernel, raw_cur, bool(extra), False, width),
            out_shape=[layer_parts[2]],
            in_specs=[VMEM] * (3 + len(extra)),
            out_specs=[VMEM],
            compiler_params=params(16),
            cost_estimate=pl.CostEstimate(flops=100_000_000, bytes_accessed=2_000_000, transcendentals=0),
            name=f"edge{n}",
        )(partial_edge, velocity_term, chip_halo, *extra)
        chip_halo = lax.ppermute(edge, "grid", chip_pairs)
        core_halo = lax.ppermute(results[0], "grid", core_pairs)
        previous, current = current, (results[0], results[1], edge)
        edge_injection = None
        if n == 0:
            spread = pl.pallas_call(
                functools.partial(inject_kernel, shots, samples, width),
                out_shape=[*layer_parts, layer_parts[0], shape(reach, rows, lanes)] + [shape(width, rows, lanes)] * (samples - 1),
                in_specs=[VMEM] * 6,
                out_specs=[VMEM] * (4 + samples),
                compiler_params=params(24),
                cost_estimate=pl.CostEstimate(flops=400_000_000, bytes_accessed=8_000_000, transcendentals=0),
                name="inject",
            )(sent, receiver_cells, *current, core_halo)
            current = tuple(spread[:3])
            core_halo, edge_injection = spread[3], spread[4]
            injections[1:] = spread[5:]


def solution(mesh):
    return jax.shard_map(
        local,
        mesh=mesh,
        in_specs=(
            P("shot", None, "grid"),
            P(None, "shot"),
            P(),
            P("grid", None, None),
            P("shot", "grid", None, None),
            P("shot", "grid", None, None),
        ),
        out_specs=(P("shot", "grid", None, None), P("shot", "grid", None, None)),
        check_vma=False,
    )
```

time: 167 us -> 61.2 us (0.37)
  other arithmetic: 61.3 us -> 0 us
  blocking collectives: 41.8 us -> 13.4 us
  local copies, waits for them, and re-layouts: 27.3 us -> 9.36 us
  Pallas kernels: 0 us -> 14.8 us
  starting transfers between devices: 22.2 us -> 11.4 us
    add x4 -> x0, other arithmetic: 44.9 us -> none  [local(): advanced = 2.0 * current - previous + velocity_term * laplace(extended)]
    unnamed x1 -> x0, blocking collectives: 30.4 us -> none
    scatter-add x4 -> x0, other arithmetic: 16.4 us -> none  [inject(): field.reshape(-1).at[flat].add(values, mode='drop').reshape(field.shape)]
    pallas_call x0 -> x10, Pallas kernels: none -> 14.8 us  [the longest x4 9.12 us: local(): pl.pallas_call(functools.partial(step_kernel, raw_cur, raw_prev, inject i...]
    all_to_all x0 -> x1, blocking collectives: none -> 13.4 us  [local(): sent = lax.all_to_all(sent, ('shot', 'grid'), 0, 0, tiled=True)]
    all_gather x1 -> x0, blocking collectives: 11.5 us -> none  [local(): traces = lax.all_gather(own_traces, 'grid', axis=1, tiled=True)]
    ppermute x8, starting transfers between devices: 22.2 us -> 11.4 us  [the longest x3 6.26 us: local(): chip_halo = lax.ppermute(edge, 'grid', chip_pairs)]
    slice x11 -> x0, local copies, waits for them, and re-layouts: 6.41 us -> none  [the longest x3 3.36 us: extended_2(): last = lax.slice_in_dim(shard, length - width, length, axis=dim)]
  transfers between devices with their start and end apart: 8 -> 8, of which waited for: 6 -> 2; matrix products, arithmetic and copies ran while one was open for 9% -> 0% of each run, Pallas kernels for 0% -> 23%
where the time goes in v1:
time: 61.2 us; the launch traced here: 60.7 us
  Pallas kernels  14.8 us (24%)
  blocking collectives  13.4 us (22%)
  starting transfers between devices  11.4 us (19%)
  waiting for transfers between devices  10.7 us (17%)
  local copies, waits for them, and re-layouts  9.36 us (15%)
  between operations  0.91 us (1%)
    all_to_all x1, blocking collectives, local(): sent = lax.all_to_all(sent, ('shot', 'grid'), 0, 0, tiled=True)  13.4 us
    ppermute x3, waiting for transfers between devices, local(): chip_halo = lax.ppermute(edge, 'grid', chip_pairs)  10.7 us
    pallas_call x4, Pallas kernels, local(): pl.pallas_call(functools.partial(step_kernel, raw_cur, raw_prev, inject i...  9.12 us
    unnamed x27, local copies, waits for them, and re-layouts  7.2 us
    ppermute x3, starting transfers between devices, local(): chip_halo = lax.ppermute(edge, 'grid', chip_pairs)  6.26 us
    ppermute x1, starting transfers between devices, local(): chip_halo = lax.ppermute(to_chip, 'grid', chip_pairs)  4.49 us
    pallas_call x1, Pallas kernels, local(): pl.pallas_call(functools.partial(inject_kernel, shots, samples, width), o...  2.87 us
    pallas_call x1, Pallas kernels, local(): pl.pallas_call(functools.partial(gather_kernel, width), out_shape=[shape(...  1.45 us
  transfers between devices with their start and end apart: 8, of which 2 were waited for; matrix products, arithmetic and copies ran while one was open for 0% of the time, Pallas kernels for 23%

profile of v1, /device:TPU:1, one launch (start us, length us, event | category | flops | bytes accessed | tf_op | source)
XLA Modules:
  0.0 60.7 jit_solution(11424909605921858863)
XLA Ops:
  0.7 1.4 %dynamic-slice_bitcast_fusion = (f32[4,128,256]{2,1,0:T(8,128)S(1)}, f32[4,128,256]{2,1,0:T(8,128)S(1)}) fusion(f32[1,16,128,256]{3,2,1,0:T(8,128)} %refs_3_.1, s32[]{:T(128)S(6)} %select_n.15, s32[]{:T(128)S(6)} %select_n.14), kind=kLoop, calls=%fused_computation | loop fusion | bytes 2097160 | tf_op jit(solution)/shard_map/dynamic_slice | solution.py:253
  2.2 4.5 %collective-permute-start.1 = (f32[4,128,256]{2,1,0:T(8,128)S(1)}, f32[4,128,256]{2,1,0:T(8,128)S(1)}, u32[]{:S(2)}, u32[]{:S(2)}) collective-permute-start(f32[4,128,256]{2,1,0:T(8,128)S(1)} %get-tuple-element.40), channel_id=1, source_target_pairs={{1,2},{2,1},{5,6},{6,5},{9,10},{10,9},{13,14},{14,13},{17,18},{18,... | collective-permute-start | bytes 1572872 | tf_op jit(solution)/shard_map/ppermute | solution.py:255
  6.7 1.6 %copy-done.2 = f32[1,16,128,256]{3,2,1,0:T(8,128)S(1)} copy-done((f32[1,16,128,256]{3,2,1,0:T(8,128)S(1)}, f32[1,16,128,256]{3,2,1,0:T(8,128)}, u32[]{:S(2)}) %copy-start.2) | copy-done | bytes 2097176
  8.3 0.9 %copy-done.4 = bf16[512,256]{1,0:T(8,128)(2,1)S(1)} copy-done((bf16[512,256]{1,0:T(8,128)(2,1)S(1)}, bf16[512,256]{1,0:T(8,128)(2,1)}, u32[]{:S(2)}) %copy-start.4) | copy-done | bytes 262168
  9.3 1.6 %copy-done.6 = f32[1,16,128,256]{3,2,1,0:T(8,128)S(1)} copy-done((f32[1,16,128,256]{3,2,1,0:T(8,128)S(1)}, f32[1,16,128,256]{3,2,1,0:T(8,128)}, u32[]{:S(2)}) %copy-start.6) | copy-done | bytes 2097176
  10.8 0.8 %copy-done.7 = bf16[128,256]{1,0:T(8,128)(2,1)S(1)} copy-done((bf16[128,256]{1,0:T(8,128)(2,1)S(1)}, bf16[128,256]{1,0:T(8,128)(2,1)}, u32[]{:S(2)}) %copy-start.7) | copy-done | bytes 65560
  11.7 2.6 %step0.1 = (f32[4,128,256]{2,1,0:T(8,128)}, f32[8,128,256]{2,1,0:T(8,128)S(1)}, f32[4,128,256]{2,1,0:T(8,128)S(1)}) custom-call(f32[1,16,128,256]{3,2,1,0:T(8,128)S(1)} %copy-done.2, f32[1,16,128,256]{3,2,1,0:T(8,128)S(1)} %copy-done.6, f32[16,128,256]{2,1,0:T(8,128)S(1)} %copy-done.1, f32[4,128,256]{2,1,0:T(8,128)S(1)} %collective-permute-done.refs_3_, ...), custom_call_target="tpu_custom_call" | custom-call | flops 900000000 | bytes 8000000 | tf_op jit(solution)/shard_map/step0/pallas_call | solution.py:271
  14.3 1.0 %copy-done.9 = f32[8,128,256]{2,1,0:T(8,128)} copy-done((f32[8,128,256]{2,1,0:T(8,128)}, f32[8,128,256]{2,1,0:T(8,128)S(1)}, u32[]{:S(2)}) %copy-start.9) | copy-done | bytes 1048600
  15.4 2.1 %collective-permute-start.3 = (f32[4,128,256]{2,1,0:T(8,128)S(1)}, f32[4,128,256]{2,1,0:T(8,128)S(1)}, u32[]{:S(2)}, u32[]{:S(2)}) collective-permute-start(f32[4,128,256]{2,1,0:T(8,128)S(1)} %edge0.1.last), channel_id=1, source_target_pairs={{1,2},{2,1},{5,6},{6,5},{9,10},{10,9},{13,14},{14,13},{17,18},{18,... | collective-permute-start | bytes 1572872 | tf_op jit(solution)/shard_map/ppermute | solution.py:314
  17.8 0.7 %all_to_all.7 = f32[32,1,512]{2,1,0:T(1,128)} reshape(f32[8,4,512]{2,1,0:T(4,128)S(1)} %broadcast_in_dim.2) | data formatting | bytes 131072 | tf_op jit(solution)/shard_map/all_to_all | solution.py:260
  18.5 13.4 %all_to_all.11 = f32[32,1,512]{2,1,0:T(1,128)S(1)} all-to-all(f32[32,1,512]{2,1,0:T(1,128)} %all_to_all.7), channel_id=1, replica_groups=mesh['shot'=8,'grid'=4] {'shot','grid'}, dimensions={0} | all-to-all | bytes 131072 | tf_op jit(solution)/shard_map/all_to_all | solution.py:260
  32.0 1.2 %copy-done.10 = f32[8,128,256]{2,1,0:T(8,128)S(1)} copy-done((f32[8,128,256]{2,1,0:T(8,128)S(1)}, f32[8,128,256]{2,1,0:T(8,128)}, u32[]{:S(2)}) %copy-start.10) | copy-done | bytes 1048600
  33.2 2.9 %inject.1 = (f32[4,128,256]{2,1,0:T(8,128)S(1)}, f32[8,128,256]{2,1,0:T(8,128)S(1)}, f32[4,128,256]{2,1,0:T(8,128)S(1)}, f32[4,128,256]{2,1,0:T(8,128)S(1)}, f32...) custom-call(f32[32,512]{1,0:T(8,128)S(1)} %bitcast.12, ...), custom_call_target="tpu_custom_call" | custom-call | flops 400000000 | bytes 8000000 | tf_op jit(solution)/shard_map/inject/pallas_call | solution.py:319
  36.1 2.0 %step1.1 = (f32[4,128,256]{2,1,0:T(8,128)S(1)}, f32[8,128,256]{2,1,0:T(8,128)S(1)}, f32[4,128,256]{2,1,0:T(8,128)S(1)}) custom-call(f32[4,128,256]{2,1,0:T(8,128)S(1)} %get-tuple-element.24.refs_0_.refs_3_, f32[8,128,256]{2,1,0:T(8,128)S(1)} %get-tuple-element.25.refs_1_.refs_4_, f32[4,128,256]{2,1,0:T(8,128)S(1)} %get-tuple-element.26.refs_2_.refs_5_, ...), custom_call_target="tpu_custom_call" | custom-call | flops 900000000 | bytes 8000000 | tf_op jit(solution)/shard_map/step1/pallas_call | solution.py:271
  38.1 0.5 collective-permute-start.4
  38.5 0.2 edge1.1.refs_2_.refs_5_
  38.7 2.1 %collective-permute-start.5 = (f32[4,128,256]{2,1,0:T(8,128)S(1)}, f32[4,128,256]{2,1,0:T(8,128)S(1)}, u32[]{:S(2)}, u32[]{:S(2)}) collective-permute-start(f32[4,128,256]{2,1,0:T(8,128)S(1)} %edge1.1.refs_2_.refs_5_), channel_id=1, source_target_pairs={{1,2},{2,1},{5,6},{6,5},{9,10},{10,9},{13,14},{14,13},{17,18},{18,... | collective-permute-start | bytes 1572872 | tf_op jit(solution)/shard_map/ppermute | solution.py:314
  40.8 2.0 %step2.1 = (f32[4,128,256]{2,1,0:T(8,128)S(1)}, f32[8,128,256]{2,1,0:T(8,128)S(1)}, f32[4,128,256]{2,1,0:T(8,128)S(1)}) custom-call(f32[4,128,256]{2,1,0:T(8,128)S(1)} %get-tuple-element.29.refs_0_.refs_3_, f32[8,128,256]{2,1,0:T(8,128)S(1)} %get-tuple-element.30.refs_1_.refs_4_, f32[4,128,256]{2,1,0:T(8,128)S(1)} %edge1.1.refs_2_.refs_5_, ...), custom_call_target="tpu_custom_call" | custom-call | flops 900000000 | bytes 8000000 | tf_op jit(solution)/shard_map/step2/pallas_call | solution.py:271
  42.8 6.4 %collective-permute-done.5.refs_2_ = f32[4,128,256]{2,1,0:T(8,128)S(1)} collective-permute-done((f32[4,128,256]{2,1,0:T(8,128)S(1)}, f32[4,128,256]{2,1,0:T(8,128)S(1)}, u32[]{:S(2)}, u32[]{:S(2)}) %collective-permute-start.5) | collective-permute-done | bytes 524320 | tf_op jit(solution)/shard_map/ppermute | solution.py:314
  49.4 2.1 %collective-permute-start.7 = (f32[4,128,256]{2,1,0:T(8,128)S(1)}, f32[4,128,256]{2,1,0:T(8,128)S(1)}, u32[]{:S(2)}, u32[]{:S(2)}) collective-permute-start(f32[4,128,256]{2,1,0:T(8,128)S(1)} %edge2.1.last.refs_2_), channel_id=1, source_target_pairs={{1,2},{2,1},{5,6},{6,5},{9,10},{10,9},{13,14},{14,13},{17,18},{18,... | collective-permute-start | bytes 1572872 | tf_op jit(solution)/shard_map/ppermute | solution.py:314
  51.4 1.4 %gather.1 = f32[1,16,128,256]{3,2,1,0:T(8,128)} custom-call(f32[4,128,256]{2,1,0:T(8,128)S(1)} %get-tuple-element.34.first.refs_0_, f32[8,128,256]{2,1,0:T(8,128)S(1)} %get-tuple-element.35.middle.refs_1_, f32[4,128,256]{2,1,0:T(8,128)S(1)} %edge2.1.last.refs_2_), custom_call_target="tpu_custom_call" | custom-call | tf_op jit(solution)/shard_map/gather/pallas_call | solution.py:295
  52.9 2.6 %step3.1 = (f32[1,16,128,256]{3,2,1,0:T(8,128)}, f32[4,128,256]{2,1,0:T(8,128)S(1)}) custom-call(f32[4,128,256]{2,1,0:T(8,128)S(1)} %get-tuple-element.34.first.refs_0_, f32[8,128,256]{2,1,0:T(8,128)S(1)} %get-tuple-element.35.middle.refs_1_, f32[4,128,256]{2,1,0:T(8,128)S(1)} %edge2.1.last.refs_2_, f32[4,128,256]{2,1,0:T(8,128)S(1)} %get-tuple-element.29.refs_0_.refs_3_, ...), custom_call_target="tpu_custom_call" | custom-call | flops 900000000 | bytes 8000000 | tf_op jit(solution)/shard_map/step3/pallas_call | solution.py:271
  55.5 4.4 %collective-permute-done.7.refs_2_ = f32[4,128,256]{2,1,0:T(8,128)S(1)} collective-permute-done((f32[4,128,256]{2,1,0:T(8,128)S(1)}, f32[4,128,256]{2,1,0:T(8,128)S(1)}, u32[]{:S(2)}, u32[]{:S(2)}) %collective-permute-start.7) | collective-permute-done | bytes 524320 | tf_op jit(solution)/shard_map/ppermute | solution.py:314
  59.9 0.9 %edge3.1 = f32[1,16,128,256]{3,2,1,0:T(8,128)} custom-call(f32[4,128,256]{2,1,0:T(8,128)S(1)} %get-tuple-element.38.refs_0_, f32[16,128,256]{2,1,0:T(8,128)S(1)} %copy-done.1, f32[4,128,256]{2,1,0:T(8,128)S(1)} %collective-permute-done.7.refs_2_, f32[1,16,128,256]{3,2,1,0:T(8,128)} %get-tuple-element.39.refs_3_), custom_call_target="tpu_custom_call", output_to_operand_aliasing={{}: (3, {})} | custom-call | tf_op jit(solution)/shard_map/edge3/pallas_call | solution.py:285
  (34 shorter events, 0.7 us)
Async XLA Ops:
  0.6 17.0 %copy-start = (bf16[8,256]{1,0:T(8,128)(2,1)S(1)}, bf16[8,256]{1,0:T(8,128)(2,1)}, u32[]{:S(2)}) copy-start(bf16[8,256]{1,0:T(8,128)(2,1)} %param.9) | copy-start | bytes 12292
  0.6 6.1 %copy-start.1 = (f32[16,128,256]{2,1,0:T(8,128)S(1)}, f32[16,128,256]{2,1,0:T(8,128)}, u32[]{:S(2)}) copy-start(f32[16,128,256]{2,1,0:T(8,128)} %refs_1_.9) | copy-start | bytes 6291460
  2.1 4.6 %collective-permute-start = (f32[4,128,256]{2,1,0:T(8,128)S(1)}, f32[4,128,256]{2,1,0:T(8,128)S(1)}, u32[]{:S(2)}, u32[]{:S(2)}) collective-permute-start(f32[4,128,256]{2,1,0:T(8,128)S(1)} %get-tuple-element.41), channel_id=1, source_target_pairs={{0,1},{1,0},{2,3},{3,2},{4,5},{5,4},{6,7},{7,6},{8,9},{9,8},{10,11... | collective-permute-start | bytes 1572872 | tf_op jit(solution)/shard_map/ppermute | solution.py:256
  2.2 13.1 %collective-permute-start.1 = (f32[4,128,256]{2,1,0:T(8,128)S(1)}, f32[4,128,256]{2,1,0:T(8,128)S(1)}, u32[]{:S(2)}, u32[]{:S(2)}) collective-permute-start(f32[4,128,256]{2,1,0:T(8,128)S(1)} %get-tuple-element.40), channel_id=1, source_target_pairs={{1,2},{2,1},{5,6},{6,5},{9,10},{10,9},{13,14},{14,13},{17,18},{18,... | collective-permute-start | bytes 1572872 | tf_op jit(solution)/shard_map/ppermute | solution.py:255
  6.7 1.6 %copy-start.2 = (f32[1,16,128,256]{3,2,1,0:T(8,128)S(1)}, f32[1,16,128,256]{3,2,1,0:T(8,128)}, u32[]{:S(2)}) copy-start(f32[1,16,128,256]{3,2,1,0:T(8,128)} %refs_3_.1) | copy-start | bytes 6291460
  8.3 0.9 %copy-start.4 = (bf16[512,256]{1,0:T(8,128)(2,1)S(1)}, bf16[512,256]{1,0:T(8,128)(2,1)}, u32[]{:S(2)}) copy-start(bf16[512,256]{1,0:T(8,128)(2,1)} %constant.29.clone.refs_4_.refs_6_.refs_8_) | copy-start | bytes 786436
  9.3 1.6 %copy-start.6 = (f32[1,16,128,256]{3,2,1,0:T(8,128)S(1)}, f32[1,16,128,256]{3,2,1,0:T(8,128)}, u32[]{:S(2)}) copy-start(f32[1,16,128,256]{3,2,1,0:T(8,128)} %refs_1_.5) | copy-start | bytes 6291460
  10.8 0.8 %copy-start.7 = (bf16[128,256]{1,0:T(8,128)(2,1)S(1)}, bf16[128,256]{1,0:T(8,128)(2,1)}, u32[]{:S(2)}) copy-start(bf16[128,256]{1,0:T(8,128)(2,1)} %constant.30.clone.refs_5_.refs_7_.refs_9_) | copy-start | bytes 196612
  14.3 1.0 %copy-start.9 = (f32[8,128,256]{2,1,0:T(8,128)}, f32[8,128,256]{2,1,0:T(8,128)S(1)}, u32[]{:S(2)}) copy-start(f32[8,128,256]{2,1,0:T(8,128)S(1)} %get-tuple-element.22.middle) | copy-start | bytes 3145732
  15.2 2.4 %copy-start.12 = (bf16[256,4,128]{2,1,0:T(4,128)(2,1)S(1)}, bf16[256,4,128]{2,1,0:T(4,128)(2,1)}, u32[]{:S(2)}) copy-start(bf16[256,4,128]{2,1,0:T(4,128)(2,1)} %param.8) | copy-start | bytes 786436
  15.2 16.7 %collective-permute-start.2 = (f32[4,128,256]{2,1,0:T(8,128)}, f32[4,128,256]{2,1,0:T(8,128)}, u32[]{:S(2)}, u32[]{:S(2)}) collective-permute-start(f32[4,128,256]{2,1,0:T(8,128)} %get-tuple-element.21.first), channel_id=1, source_target_pairs={{0,1},{1,0},{2,3},{3,2},{4,5},{5,4},{6,7},{7,6},{8,9},{9,8},{10,11... | collective-permute-start | bytes 1572872 | tf_op jit(solution)/shard_map/ppermute | solution.py:315
  15.3 16.7 %copy-start.11 = (s32[3,512]{1,0:T(4,128)S(1)}, s32[3,512]{1,0:T(4,128)}, u32[]{:S(2)}) copy-start(s32[3,512]{1,0:T(4,128)} %cells.1) | copy-start | bytes 18436
  15.4 20.7 %copy-start.5 = (bf16[512,256]{1,0:T(8,128)(2,1)S(1)}, bf16[512,256]{1,0:T(8,128)(2,1)}, u32[]{:S(2)}) copy-start(bf16[512,256]{1,0:T(8,128)(2,1)} %constant.29.clone.refs_4_.refs_6_.refs_8_) | copy-start | bytes 786436
  15.4 20.7 %copy-start.8 = (bf16[128,256]{1,0:T(8,128)(2,1)S(1)}, bf16[128,256]{1,0:T(8,128)(2,1)}, u32[]{:S(2)}) copy-start(bf16[128,256]{1,0:T(8,128)(2,1)} %constant.30.clone.refs_5_.refs_7_.refs_9_) | copy-start | bytes 196612
  15.4 23.1 %collective-permute-start.3 = (f32[4,128,256]{2,1,0:T(8,128)S(1)}, f32[4,128,256]{2,1,0:T(8,128)S(1)}, u32[]{:S(2)}, u32[]{:S(2)}) collective-permute-start(f32[4,128,256]{2,1,0:T(8,128)S(1)} %edge0.1.last), channel_id=1, source_target_pairs={{1,2},{2,1},{5,6},{6,5},{9,10},{10,9},{13,14},{14,13},{17,18},{18,... | collective-permute-start | bytes 1572872 | tf_op jit(solution)/shard_map/ppermute | solution.py:314
  18.5 17.6 %copy-start.3 = (f32[1,16,128,256]{3,2,1,0:T(8,128)S(1)}, f32[1,16,128,256]{3,2,1,0:T(8,128)}, u32[]{:S(2)}) copy-start(f32[1,16,128,256]{3,2,1,0:T(8,128)} %refs_3_.1) | copy-start | bytes 6291460
  32.0 1.2 %copy-start.10 = (f32[8,128,256]{2,1,0:T(8,128)S(1)}, f32[8,128,256]{2,1,0:T(8,128)}, u32[]{:S(2)}) copy-start(f32[8,128,256]{2,1,0:T(8,128)} %copy-done.9) | copy-start | bytes 3145732
  38.1 2.7 %collective-permute-start.4 = (f32[4,128,256]{2,1,0:T(8,128)S(1)}, f32[4,128,256]{2,1,0:T(8,128)S(1)}, u32[]{:S(2)}, u32[]{:S(2)}) collective-permute-start(f32[4,128,256]{2,1,0:T(8,128)S(1)} %get-tuple-element.29.refs_0_.refs_3_), channel_id=1, source_target_pairs={{0,1},{1,0},{2,3},{3,2},{4,5},{5,4},{6,7},{7,6},{8,9},{9,8},{10,11... | collective-permute-start | bytes 1572872 | tf_op jit(solution)/shard_map/ppermute | solution.py:315
  38.7 10.5 %collective-permute-start.5 = (f32[4,128,256]{2,1,0:T(8,128)S(1)}, f32[4,128,256]{2,1,0:T(8,128)S(1)}, u32[]{:S(2)}, u32[]{:S(2)}) collective-permute-start(f32[4,128,256]{2,1,0:T(8,128)S(1)} %edge1.1.refs_2_.refs_5_), channel_id=1, source_target_pairs={{1,2},{2,1},{5,6},{6,5},{9,10},{10,9},{13,14},{14,13},{17,18},{18,... | collective-permute-start | bytes 1572872 | tf_op jit(solution)/shard_map/ppermute | solution.py:314
  42.8 10.1 %collective-permute-start.6 = (f32[4,128,256]{2,1,0:T(8,128)S(1)}, f32[4,128,256]{2,1,0:T(8,128)S(1)}, u32[]{:S(2)}, u32[]{:S(2)}) collective-permute-start(f32[4,128,256]{2,1,0:T(8,128)S(1)} %get-tuple-element.34.first.refs_0_), channel_id=1, source_target_pairs={{0,1},{1,0},{2,3},{3,2},{4,5},{5,4},{6,7},{7,6},{8,9},{9,8},{10,11... | collective-permute-start | bytes 1572872 | tf_op jit(solution)/shard_map/ppermute | solution.py:315
  49.4 10.5 %collective-permute-start.7 = (f32[4,128,256]{2,1,0:T(8,128)S(1)}, f32[4,128,256]{2,1,0:T(8,128)S(1)}, u32[]{:S(2)}, u32[]{:S(2)}) collective-permute-start(f32[4,128,256]{2,1,0:T(8,128)S(1)} %edge2.1.last.refs_2_), channel_id=1, source_target_pairs={{1,2},{2,1},{5,6},{6,5},{9,10},{10,9},{13,14},{14,13},{17,18},{18,... | collective-permute-start | bytes 1572872 | tf_op jit(solution)/shard_map/ppermute | solution.py:314

commit v2 on v0

v2 whole, which is shorter than its diff:
```python
import functools

import jax
import jax.numpy as jnp
from jax import lax
from jax.experimental import pallas as pl
from jax.experimental.pallas import tpu as pltpu
from jax.sharding import PartitionSpec as P

scale = 5040.0
weights = (-14350.0, 8064.0, -1008.0, 128.0, -9.0)
coeffs = tuple(w / scale for w in weights)
reach = 4
near = 8
lanes = 128
chunk = 32
f32 = jnp.float32
bf16 = jnp.bfloat16

VMEM = pl.BlockSpec(memory_space=pltpu.VMEM)
HBM = pl.BlockSpec(memory_space=pltpu.HBM)


def odd_device():
    return lax.rem(lax.axis_index("grid"), 2)


def place(u, width):
    odd = odd_device()
    return odd * u + (1 - odd) * (width - 1 - u)


def raw_of(ref, u):
    at = place(u, ref.shape[-3])
    return ref.at[0, at] if len(ref.shape) == 4 else ref.at[at]


def slice_of(ref, u, mine, low=0):
    flip = odd_device() if mine else 1 - odd_device()
    return ref.at[low + flip * u + (1 - flip) * (reach - 1 - u)]


def part_of(parts, u):
    first, middle, last = parts
    if u < reach:
        return first.at[u]
    if u < reach + middle.shape[0]:
        return middle.at[u - reach]
    return last.at[u - reach - middle.shape[0]]


def band(size):
    offset = jnp.abs(lax.broadcasted_iota(jnp.int32, (size, size), 0) - lax.broadcasted_iota(jnp.int32, (size, size), 1))
    table = jnp.zeros((size, size), f32)
    for j in range(1, reach + 1):
        table = jnp.where(offset == j, weights[j], table)
    return table.astype(bf16)


def chunks(rows):
    return [pl.ds(at, min(chunk, rows - at)) for at in range(0, rows, chunk)]


def step_kernel(kind, width, *refs):
    refs = list(refs)
    take = lambda n: tuple(refs.pop(0) for _ in range(n))
    cur_parts = take(1 if kind == "start" else 3)
    prev_parts = take(1 if kind in ("start", "full") else 3)
    velocity, core_halo = take(2)
    inject = None if kind == "start" else take(1)[0]
    chip_halo = take(1)[0] if kind == "full" else None
    outs = take(2 if kind == "final" else 3)
    sums, zband, yband = take(3)
    rows, depth = velocity.shape[1], velocity.shape[2]

    def cur(u):
        if u < 0:
            return slice_of(core_halo, -1 - u, False) if kind == "start" else core_halo.at[-1 - u]
        if u >= width:
            return chip_halo.at[reach - 1 - (u - width)]
        return raw_of(cur_parts[0], u) if kind == "start" else part_of(cur_parts, u)

    def prev(u):
        return raw_of(prev_parts[0], u) if kind in ("start", "full") else part_of(prev_parts, u)

    if kind == "final":
        whole, last = outs
        ready, sem = take(2)

        def out(u):
            return ready.at[u] if u < width - reach else last.at[u - width + reach]

        def copy(u):
            return pltpu.make_async_copy(ready.at[u], raw_of(whole, u), sem.at[u])
    else:

        def out(u):
            return part_of(outs, u)

    along = band(depth)
    zband[:depth, :] = along
    zband[depth:, :] = along
    across = band(rows)
    yband[:, :rows] = across
    yband[:, rows:] = across
    for u in range(width):
        field = cur(u)[...]
        high = field.astype(bf16)
        low = (field - high.astype(f32)).astype(bf16)
        along_z = jnp.dot(jnp.concatenate([high, low], axis=1), zband[...], preferred_element_type=f32)
        along_y = jnp.dot(yband[...], jnp.concatenate([high, low], axis=0), preferred_element_type=f32)
        sums[u] = along_y + along_z
        for part in chunks(rows):
            here = cur(u)[part, :]
            total = sums[u, part, :] * (1.0 / scale) + (3.0 * coeffs[0]) * here
            for j in range(1, reach + 1):
                pair = cur(u - j)[part, :]
                if u + j < width or chip_halo is not None:
                    pair = pair + cur(u + j)[part, :]
                total = total + coeffs[j] * pair
            result = (here + here) - prev(u)[part, :] + raw_of(velocity, u)[part, :] * total
            out(u)[part, :] = result
            if inject is not None:
                out(u)[part, :lanes] = result[:, :lanes] + inject[u, part, :]
        if kind == "final" and 1 <= u <= width - reach:
            copy(u - 1).start()
    if kind == "final":
        for u in range(width - reach):
            copy(u).wait()


def edge_value(partial, factor, halo, i, part):
    total = None
    for j in range(reach - i, reach + 1):
        term = coeffs[j] * halo(reach - 1 - (i + j - reach))[part, :]
        total = term if total is None else total + term
    return partial[part, :] + factor[part, :] * total


def edge_kernel(width, partial, velocity, halo, out):
    for i in range(reach):
        for part in chunks(velocity.shape[1]):
            out[i, part, :] = edge_value(partial.at[i], raw_of(velocity, width - reach + i), lambda k: halo.at[k], i, part)


def last_edge_kernel(width, partial, velocity, halo_partial, halo_velocity, own, whole_in, whole, halo, result, sem):
    def copy(i):
        return pltpu.make_async_copy(result.at[i], raw_of(whole, width - reach + i), sem.at[i])

    parts = chunks(velocity.shape[1])
    for i in range(reach):
        for part in parts:
            halo[i, part, :] = edge_value(halo_partial.at[i], slice_of(halo_velocity, i, False, reach), lambda k: own.at[k], i, part)
    for i in range(reach):
        for part in parts:
            result[i, part, :] = edge_value(partial.at[i], raw_of(velocity, width - reach + i), lambda k: halo.at[k], i, part)
        if i >= 1:
            copy(i - 1).start()
    copy(reach - 1).start()
    for i in range(reach):
        copy(i).wait()


def fan_kernel(groups, partial, out):
    for k in range(partial.shape[0]):
        for g in range(groups):
            out[k * groups + g] = partial[k : k + 1, :]


def spread_traces(steps, shots, samples, width, rows, sent, cells):
    groups = sent.shape[0] // shots
    own = sent.shape[2] // samples
    start = lax.axis_index("grid") * width
    traces = []
    for g in range(groups):
        row = sent[g]
        for s in range(1, shots):
            row = row + sent[s * groups + g]
        traces.append(row)
    totals = {}
    per = max(1, 512 // own)
    for g0 in range(0, groups, per):
        gs = range(g0, min(groups, g0 + per))
        span = slice(g0 * own, (gs[-1] + 1) * own)
        u = place(cells[0:1, span] - start, width)
        y, z = cells[1:2, span], cells[2:3, span]
        count = y.shape[1]
        at_row = jnp.where(lax.broadcasted_iota(jnp.int32, (rows, count), 0) == y, 1.0, 0.0).astype(bf16)
        at_row = jnp.concatenate([at_row, at_row], axis=1)
        for n in steps:
            t = samples - 1 - n
            value = jnp.concatenate([traces[g][:, t * own : (t + 1) * own] for g in gs], axis=1)
            low_u = -reach if n == 0 else 0
            size = (width - 2 * low_u) * near
            inside = (u >= low_u) & (u < width - low_u)
            cell = jnp.where(inside, (u - low_u) * near + z, -1)
            weighted = jnp.where(lax.broadcasted_iota(jnp.int32, (size, count), 0) == cell, value, 0.0)
            high = weighted.astype(bf16)
            rest = (weighted - high.astype(f32)).astype(bf16)
            both = jnp.concatenate([high, rest], axis=1)
            out = lax.dot_general(at_row, both, (((1,), (1,)), ((), ())), preferred_element_type=f32)
            totals[n] = totals[n] + out if n in totals else out
    inside = lax.broadcasted_iota(jnp.int32, (rows, lanes), 1) < near

    def layer(n, u):
        at = (u + (reach if n == 0 else 0)) * near
        base = at // lanes * lanes
        tile = totals[n][:, base : base + lanes]
        if tile.shape[1] < lanes:
            tile = jnp.concatenate([tile, jnp.zeros((rows, lanes - tile.shape[1]), f32)], axis=1)
        moved = pltpu.roll(tile, lanes - (at - base), 1) if at > base else tile
        return jnp.where(inside, moved, 0.0)

    return layer


def inject_kernel(shots, samples, width, sent, cells, first, middle, partial, core_halo, velocity, chip_in, chip_partial, chip_own, *outs):
    o_first, o_middle, o_last, o_core, o_chip, o_step = outs
    rows = first.shape[1]
    layer = spread_traces((0, 1), shots, samples, width, rows, sent, cells)
    for i in range(reach):
        for part in chunks(rows):
            o_last[i, part, :] = edge_value(partial.at[i], raw_of(velocity, width - reach + i), lambda k: slice_of(chip_in, k, False), i, part)
            o_chip[i, part, :] = edge_value(chip_partial.at[i], slice_of(chip_in, i, False, reach), lambda k: slice_of(chip_own, k, True), i, part)
    for u in range(-reach, width + reach):
        extra = layer(0, u)
        if u >= width - reach:
            target = o_chip.at[reach - 1 - (u - width)] if u >= width else o_last.at[u - width + reach]
            target[:, :lanes] = target[:, :lanes] + extra
            continue
        if u < 0:
            source, target = core_halo.at[-1 - u], o_core.at[-1 - u]
        else:
            source, target = part_of((first, middle, None), u), part_of((o_first, o_middle, None), u)
        target[:, lanes:] = source[:, lanes:]
        target[:, :lanes] = source[:, :lanes] + extra
    for u in range(width):
        o_step[u] = layer(1, u)


def spread_kernel(steps, shots, samples, width, sent, cells, *outs):
    layer = spread_traces(steps, shots, samples, width, outs[0].shape[1], sent, cells)
    for n, out in zip(steps, outs):
        for u in range(width):
            out[u] = layer(n, u)


def gather_kernel(width, first, middle, last, whole, sem):
    copies = [pltpu.make_async_copy(part_of((first, middle, last), u), raw_of(whole, u), sem.at[u]) for u in range(width)]
    for copy in copies:
        copy.start()
    for copy in copies:
        copy.wait()


def call(kernel, name, ins, outs, scratch=(), in_hbm=(), out_hbm=(), mib=16, flops=100_000_000, aliases={}):
    return pl.pallas_call(
        kernel,
        out_shape=outs,
        in_specs=[HBM if k in in_hbm else VMEM for k in range(len(ins))],
        out_specs=[HBM if k in out_hbm else VMEM for k in range(len(outs))],
        scratch_shapes=list(scratch),
        input_output_aliases=aliases,
        compiler_params=pltpu.CompilerParams(vmem_limit_bytes=mib * 1024 * 1024),
        cost_estimate=pl.CostEstimate(flops=flops, bytes_accessed=1_000_000, transcendentals=0),
        name=name,
    )(*ins)


def local(residuals, encoding, receiver_cells, velocity, field_before, field_start):
    shot_rows, samples, own = residuals.shape
    width, rows, depth = velocity.shape
    groups, shots = lax.axis_size("grid"), lax.axis_size("shot")
    assert samples == 4 and width >= 2 * reach
    shape = lambda *s: jax.ShapeDtypeStruct(s, f32)
    four, whole, small = shape(reach, rows, depth), shape(1, width, rows, depth), shape(width, rows, lanes)
    parts = [four, shape(width - 2 * reach, rows, depth), four]
    core_pairs = [(i, i ^ 1) for i in range(groups) if i ^ 1 < groups]
    chip_pairs = [(i, j) for i in range(groups) for j in [((i + 1) ^ 1) - 1] if 0 <= j < groups]
    to_core = lambda x: lax.ppermute(x, "grid", core_pairs)
    to_chip = lambda x: lax.ppermute(x, "grid", chip_pairs)
    sums = pltpu.VMEM((width, rows, depth), f32)
    bands = [pltpu.VMEM((2 * depth, depth), bf16), pltpu.VMEM((rows, 2 * rows), bf16)]
    dma = pltpu.SemaphoreType.DMA
    step = lambda kind: functools.partial(step_kernel, kind, width)
    work = 900_000_000

    odd = odd_device()
    toward_chip = lambda x: lax.dynamic_slice_in_dim(x, odd * (width - reach), reach, 0)
    core_own = lax.dynamic_slice_in_dim(field_start[0], (1 - odd) * (width - reach), reach, 0)
    chip_own = jnp.concatenate([toward_chip(field_start[0]), toward_chip(velocity)], axis=0)
    core_halo = to_core(core_own)
    chip_in = to_chip(chip_own)
    first, middle, partial = call(
        step("start"), "step0", (field_start, field_before, velocity, core_halo), parts,
        [sums, *bands], flops=work,
    )
    core_halo = to_core(first)
    chip_partial = to_chip(partial)

    summed = jnp.dot(encoding, residuals.reshape(shot_rows, samples * own), preferred_element_type=f32)
    summed, _ = lax.optimization_barrier((summed, partial))
    (sent,) = call(functools.partial(fan_kernel, groups), "fan", (summed,), [shape(shots * groups, 1, samples * own)], mib=4)
    sent = lax.all_to_all(sent, ("shot", "grid"), 0, 0, tiled=True)

    *before, core_halo, chip_halo, source = call(
        functools.partial(inject_kernel, shots, samples, width), "inject",
        (sent, receiver_cells, first, middle, partial, core_halo, velocity, chip_in, chip_partial, chip_own),
        [*parts, four, four, small], flops=work,
    )
    current = call(
        step("full"), "step1", (*before, field_start, velocity, core_halo, source, chip_halo), parts, [sums, *bands], flops=work
    )
    core_halo = to_core(current[0])
    chip_halo = to_chip(current[2])
    sent, core_halo = lax.optimization_barrier((sent, core_halo))
    sources = call(
        functools.partial(spread_kernel, (2, 3), shots, samples, width), "spread", (sent, receiver_cells), [small, small], flops=work // 2
    )
    first, middle, partial = call(
        step("part"), "step2", (*current, *before, velocity, core_halo, sources[0]), parts, [sums, *bands], flops=work
    )
    core_halo = to_core(first)
    chip_partial = to_chip(partial)
    (last,) = call(functools.partial(edge_kernel, width), "edge", (partial, velocity, chip_halo), [four])
    end, partial = call(
        step("final"), "step3", (first, middle, last, *current, velocity, core_halo, sources[1]), [whole, four],
        [sums, *bands, pltpu.VMEM((width - reach, rows, depth), f32), dma((width - reach,))], out_hbm=(0,), flops=work,
    )
    (stored,) = call(functools.partial(gather_kernel, width), "gather", (first, middle, last), [whole], [dma((width,))], out_hbm=(0,))
    (end,) = call(
        functools.partial(last_edge_kernel, width), "last_edge", (partial, velocity, chip_partial, chip_in, current[2], end), [whole],
        [pltpu.VMEM((reach, rows, depth), f32), pltpu.VMEM((reach, rows, depth), f32), dma((reach,))], (5,), (0,), aliases={5: 0},
    )
    return stored, end


def solution(mesh):
    return jax.shard_map(
        local,
        mesh=mesh,
        in_specs=(
            P("shot", None, "grid"),
            P(None, "shot"),
            P(),
            P("grid", None, None),
            P("shot", "grid", None, None),
            P("shot", "grid", None, None),
        ),
        out_specs=(P("shot", "grid", None, None), P("shot", "grid", None, None)),
        check_vma=False,
    )
```

time: 167 us -> 49 us (0.29)
  other arithmetic: 61.3 us -> 0.07 us
  blocking collectives: 41.8 us -> 14 us
  local copies, waits for them, and re-layouts: 27.3 us -> 3.44 us
  Pallas kernels: 0 us -> 13.7 us
  starting transfers between devices: 22.2 us -> 13.2 us
  waiting for transfers between devices: 12 us -> 3.39 us
    add x4 -> x0, other arithmetic: 44.9 us -> none  [local(): advanced = 2.0 * current - previous + velocity_term * laplace(extended)]
    unnamed x1 -> x0, blocking collectives: 30.4 us -> none
    scatter-add x4 -> x0, other arithmetic: 16.4 us -> none  [inject(): field.reshape(-1).at[flat].add(values, mode='drop').reshape(field.shape)]
    all_to_all x0 -> x1, blocking collectives: none -> 14 us  [local(): sent = lax.all_to_all(sent, ('shot', 'grid'), 0, 0, tiled=True)]
    pallas_call x0 -> x10, Pallas kernels: none -> 13.7 us  [call(): pl.pallas_call(kernel, out_shape=outs, in_specs=[HBM if k in in_hbm else...]
    all_gather x1 -> x0, blocking collectives: 11.5 us -> none  [local(): traces = lax.all_gather(own_traces, 'grid', axis=1, tiled=True)]
    unnamed x44 -> x12, local copies, waits for them, and re-layouts: 12.2 us -> 1.95 us
    ppermute x8, starting transfers between devices: 22.2 us -> 13.2 us  [the longest x4 12.1 us: local(): to_chip = lambda x: lax.ppermute(x, 'grid', chip_pairs)]
  transfers between devices with their start and end apart: 8 -> 8, of which waited for: 6 -> 2; matrix products, arithmetic and copies ran while one was open for 9% -> 1% of each run, Pallas kernels for 0% -> 19%
where the time goes in v2:
time: 49 us; the launch traced here: 48.8 us
  blocking collectives  14 us (29%)
  Pallas kernels  13.7 us (28%)
  starting transfers between devices  13.2 us (27%)
  local copies, waits for them, and re-layouts  3.44 us (7%)
  waiting for transfers between devices  3.39 us (7%)
  between operations  0.88 us (2%)
    all_to_all x1, blocking collectives, local(): sent = lax.all_to_all(sent, ('shot', 'grid'), 0, 0, tiled=True)  14 us
    pallas_call x10, Pallas kernels, call(): pl.pallas_call(kernel, out_shape=outs, in_specs=[HBM if k in in_hbm else...  13.7 us
    ppermute x4, starting transfers between devices, local(): to_chip = lambda x: lax.ppermute(x, 'grid', chip_pairs)  12.1 us
    ppermute x4, waiting for transfers between devices, local(): to_chip = lambda x: lax.ppermute(x, 'grid', chip_pairs)  3.37 us
    unnamed x12, local copies, waits for them, and re-layouts  1.95 us
    dynamic_slice x2, local copies, waits for them, and re-layouts, local(): lax.dynamic_slice_in_dim(x, odd * (width - reach), reach, 0)  1.49 us
    ppermute x4, starting transfers between devices, local(): to_core = lambda x: lax.ppermute(x, 'grid', core_pairs)  1.05 us
  transfers between devices with their start and end apart: 8, of which 2 were waited for; matrix products, arithmetic and copies ran while one was open for 1% of the time, Pallas kernels for 19%

profile of v2, /device:TPU:1, one launch (start us, length us, event | category | flops | bytes accessed | tf_op | source)
XLA Modules:
  0.0 48.8 jit_solution(5038628646744943249)
XLA Ops:
  0.7 1.5 %dynamic-slice_bitcast_fusion = (f32[4,128,256]{2,1,0:T(8,128)S(1)}, f32[4,128,256]{2,1,0:T(8,128)S(1)}) fusion(f32[1,16,128,256]{3,2,1,0:T(8,128)} %refs_3_.1, s32[]{:T(128)S(6)} %select_n.8, s32[]{:T(128)S(6)} %select_n.7), kind=kLoop, calls=%fused_computation.1 | loop fusion | bytes 2097160 | tf_op jit(solution)/shard_map/dynamic_slice | solution.py:289
  2.1 0.1 collective-permute-start
  2.2 0.3 copy-done.1
  2.7 4.6 %collective-permute-start.2 = (f32[8,128,256]{2,1,0:T(8,128)S(1)}, f32[8,128,256]{2,1,0:T(8,128)S(1)}, u32[]{:S(2)}, u32[]{:S(2)}) collective-permute-start(f32[8,128,256]{2,1,0:T(8,128)S(1)} %pad_maximum_fusion.chip_own), channel_id=1, source_target_pairs={{1,2},{2,1},{5,6},{6,5},{9,10},{10,9},{13,14},{14,13},{17,18},{18,... | collective-permute-start | bytes 3145736 | tf_op jit(solution)/shard_map/ppermute | solution.py:281
  7.4 1.6 %copy-done.3 = f32[1,16,128,256]{3,2,1,0:T(8,128)S(1)} copy-done((f32[1,16,128,256]{3,2,1,0:T(8,128)S(1)}, f32[1,16,128,256]{3,2,1,0:T(8,128)}, u32[]{:S(2)}) %copy-start.3) | copy-done | bytes 2097176
  9.0 2.1 %step0.1 = (f32[4,128,256]{2,1,0:T(8,128)S(1)}, f32[8,128,256]{2,1,0:T(8,128)S(1)}, f32[4,128,256]{2,1,0:T(8,128)S(1)}) custom-call(f32[1,16,128,256]{3,2,1,0:T(8,128)S(1)} %copy-done.2, f32[1,16,128,256]{3,2,1,0:T(8,128)S(1)} %copy-done.3, f32[16,128,256]{2,1,0:T(8,128)S(1)} %copy-done.1, f32[4,128,256]{2,1,0:T(8,128)S(1)} %collective-permute-done.refs_3_), custom_call_target="tpu_custom_call" | custom-call | flops 900000000 | bytes 1000000 | tf_op jit(solution)/shard_map/step0/pallas_call | solution.py:257
  11.0 0.1 collective-permute-start.1
  11.1 1.9 %collective-permute-start.3 = (f32[4,128,256]{2,1,0:T(8,128)S(1)}, f32[4,128,256]{2,1,0:T(8,128)S(1)}, u32[]{:S(2)}, u32[]{:S(2)}) collective-permute-start(f32[4,128,256]{2,1,0:T(8,128)S(1)} %get-tuple-element.24.partial), channel_id=1, source_target_pairs={{1,2},{2,1},{5,6},{6,5},{9,10},{10,9},{13,14},{14,13},{17,18},{18,... | collective-permute-start | bytes 1572872 | tf_op jit(solution)/shard_map/ppermute | solution.py:281
  13.0 0.1 fusion.partial
  13.2 14.0 %all_to_all.5.sent = f32[32,1,512]{2,1,0:T(1,128)S(1)} all-to-all(f32[32,1,512]{2,1,0:T(1,128)S(1)} %fan.1), channel_id=1, replica_groups=mesh['shot'=8,'grid'=4] {'shot','grid'}, dimensions={0} | all-to-all | bytes 131072 | tf_op jit(solution)/shard_map/all_to_all | solution.py:304
  27.2 1.2 %inject.1 = (f32[4,128,256]{2,1,0:T(8,128)S(1)}, f32[8,128,256]{2,1,0:T(8,128)S(1)}, f32[4,128,256]{2,1,0:T(8,128)S(1)}, f32[4,128,256]{2,1,0:T(8,128)S(1)}, f32...) custom-call(f32[32,1,512]{2,1,0:T(1,128)S(1)} %all_to_all.5.sent, s32[3,512]{1,0:T(4,128)S(1)} %copy-done.4, ...), custom_call_target="tpu_custom_call" | custom-call | flops 900000000 | bytes 1000000 | tf_op jit(solution)/shard_map/inject/pallas_call | solution.py:257
  28.4 2.1 %step1.1 = (f32[4,128,256]{2,1,0:T(8,128)S(1)}, f32[8,128,256]{2,1,0:T(8,128)S(1)}, f32[4,128,256]{2,1,0:T(8,128)S(1)}) custom-call(f32[4,128,256]{2,1,0:T(8,128)S(1)} %get-tuple-element.28.refs_0_.refs_3_, f32[8,128,256]{2,1,0:T(8,128)S(1)} %get-tuple-element.29.refs_1_.refs_4_, f32[4,128,256]{2,1,0:T(8,128)S(1)} %get-tuple-element.30.refs_2_.refs_5_, ...), custom_call_target="tpu_custom_call" | custom-call | flops 900000000 | bytes 1000000 | tf_op jit(solution)/shard_map/step1/pallas_call | solution.py:257
  30.6 0.8 %collective-permute-start.4 = (f32[4,128,256]{2,1,0:T(8,128)S(1)}, f32[4,128,256]{2,1,0:T(8,128)S(1)}, u32[]{:S(2)}, u32[]{:S(2)}) collective-permute-start(f32[4,128,256]{2,1,0:T(8,128)S(1)} %get-tuple-element.34.refs_0_.refs_3_), channel_id=1, source_target_pairs={{0,1},{1,0},{2,3},{3,2},{4,5},{5,4},{6,7},{7,6},{8,9},{9,8},{10,11... | collective-permute-start | bytes 1572872 | tf_op jit(solution)/shard_map/ppermute | solution.py:280
  31.4 2.8 %collective-permute-start.5 = (f32[4,128,256]{2,1,0:T(8,128)S(1)}, f32[4,128,256]{2,1,0:T(8,128)S(1)}, u32[]{:S(2)}, u32[]{:S(2)}) collective-permute-start(f32[4,128,256]{2,1,0:T(8,128)S(1)} %get-tuple-element.36.refs_2_.refs_5_.own), channel_id=1, source_target_pairs={{1,2},{2,1},{5,6},{6,5},{9,10},{10,9},{13,14},{14,13},{17,18},{18,... | collective-permute-start | bytes 1572872 | tf_op jit(solution)/shard_map/ppermute | solution.py:281
  34.3 0.9 %spread.1 = (f32[16,128,128]{2,1,0:T(8,128)S(1)}, f32[16,128,128]{2,1,0:T(8,128)S(1)}) custom-call(f32[32,1,512]{2,1,0:T(1,128)S(1)} %all_to_all.5.sent, s32[3,512]{1,0:T(4,128)S(1)} %copy-done.4), custom_call_target="tpu_custom_call" | custom-call | flops 450000000 | bytes 1000000 | tf_op jit(solution)/shard_map/spread/pallas_call | solution.py:257
  35.1 2.0 %step2.1 = (f32[4,128,256]{2,1,0:T(8,128)S(1)}, f32[8,128,256]{2,1,0:T(8,128)S(1)}, f32[4,128,256]{2,1,0:T(8,128)S(1)}) custom-call(f32[4,128,256]{2,1,0:T(8,128)S(1)} %get-tuple-element.34.refs_0_.refs_3_, f32[8,128,256]{2,1,0:T(8,128)S(1)} %get-tuple-element.35.refs_1_.refs_4_, f32[4,128,256]{2,1,0:T(8,128)S(1)} %get-tuple-element.36.refs_2_.refs_5_.own, ...), custom_call_target="tpu_custom_call" | custom-call | flops 900000000 | bytes 1000000 | tf_op jit(solution)/shard_map/step2/pallas_call | solution.py:257
  37.2 0.1 collective-permute-start.6
  37.3 2.7 %collective-permute-start.7 = (f32[4,128,256]{2,1,0:T(8,128)S(1)}, f32[4,128,256]{2,1,0:T(8,128)S(1)}, u32[]{:S(2)}, u32[]{:S(2)}) collective-permute-start(f32[4,128,256]{2,1,0:T(8,128)S(1)} %get-tuple-element.42.partial), channel_id=1, source_target_pairs={{1,2},{2,1},{5,6},{6,5},{9,10},{10,9},{13,14},{14,13},{17,18},{18,... | collective-permute-start | bytes 1572872 | tf_op jit(solution)/shard_map/ppermute | solution.py:281
  40.0 1.9 %collective-permute-done.5.halo = f32[4,128,256]{2,1,0:T(8,128)S(1)} collective-permute-done((f32[4,128,256]{2,1,0:T(8,128)S(1)}, f32[4,128,256]{2,1,0:T(8,128)S(1)}, u32[]{:S(2)}, u32[]{:S(2)}) %collective-permute-start.5) | collective-permute-done | bytes 524320 | tf_op jit(solution)/shard_map/ppermute | solution.py:281
  41.9 0.1 edge.1.last.refs_2_
  42.0 1.4 %gather.1 = f32[1,16,128,256]{3,2,1,0:T(8,128)} custom-call(f32[4,128,256]{2,1,0:T(8,128)S(1)} %get-tuple-element.40.first.refs_0_, f32[8,128,256]{2,1,0:T(8,128)S(1)} %get-tuple-element.41.middle.refs_1_, f32[4,128,256]{2,1,0:T(8,128)S(1)} %edge.1.last.refs_2_), custom_call_target="tpu_custom_call" | custom-call | flops 100000000 | bytes 1000000 | tf_op jit(solution)/shard_map/gather/pallas_call | solution.py:257
  43.5 2.8 %step3.1 = (f32[1,16,128,256]{3,2,1,0:T(8,128)}, f32[4,128,256]{2,1,0:T(8,128)S(1)}) custom-call(f32[4,128,256]{2,1,0:T(8,128)S(1)} %get-tuple-element.40.first.refs_0_, f32[8,128,256]{2,1,0:T(8,128)S(1)} %get-tuple-element.41.middle.refs_1_, f32[4,128,256]{2,1,0:T(8,128)S(1)} %edge.1.last.refs_2_, f32[4,128,256]{2,1,0:T(8,128)S(1)} %get-tuple-element.34.refs_0_.refs_3_, ...), custom_call_target="tpu_custom_call" | custom-call | flops 900000000 | bytes 1000000 | tf_op jit(solution)/shard_map/step3/pallas_call | solution.py:257
  46.3 1.5 %collective-permute-done.7.halo_partial = f32[4,128,256]{2,1,0:T(8,128)S(1)} collective-permute-done((f32[4,128,256]{2,1,0:T(8,128)S(1)}, f32[4,128,256]{2,1,0:T(8,128)S(1)}, u32[]{:S(2)}, u32[]{:S(2)}) %collective-permute-start.7) | collective-permute-done | bytes 524320 | tf_op jit(solution)/shard_map/ppermute | solution.py:281
  47.8 1.0 %last_edge.1 = f32[1,16,128,256]{3,2,1,0:T(8,128)} custom-call(f32[4,128,256]{2,1,0:T(8,128)S(1)} %get-tuple-element.44.partial, f32[16,128,256]{2,1,0:T(8,128)S(1)} %copy-done.1, f32[4,128,256]{2,1,0:T(8,128)S(1)} %collective-permute-done.7.halo_partial, ...), custom_call_target="tpu_custom_call", output_to_operand_aliasing={{}: (5, {})} | custom-call | flops 100000000 | bytes 1000000 | tf_op jit(solution)/shard_map/last_edge/pallas_call | solution.py:257
  (19 shorter events, 0.2 us)
Async XLA Ops:
  0.6 12.4 %copy-start = (bf16[8,256]{1,0:T(8,128)(2,1)S(1)}, bf16[8,256]{1,0:T(8,128)(2,1)}, u32[]{:S(2)}) copy-start(bf16[8,256]{1,0:T(8,128)(2,1)} %param.7) | copy-start | bytes 12292
  0.6 1.9 %copy-start.1 = (f32[16,128,256]{2,1,0:T(8,128)S(1)}, f32[16,128,256]{2,1,0:T(8,128)}, u32[]{:S(2)}) copy-start(f32[16,128,256]{2,1,0:T(8,128)} %velocity.5) | copy-start | bytes 6291460
  2.1 5.2 %copy-start.2 = (f32[1,16,128,256]{3,2,1,0:T(8,128)S(1)}, f32[1,16,128,256]{3,2,1,0:T(8,128)}, u32[]{:S(2)}) copy-start(f32[1,16,128,256]{3,2,1,0:T(8,128)} %refs_3_.1) | copy-start | bytes 6291460
  2.1 5.2 %collective-permute-start = (f32[4,128,256]{2,1,0:T(8,128)S(1)}, f32[4,128,256]{2,1,0:T(8,128)S(1)}, u32[]{:S(2)}, u32[]{:S(2)}) collective-permute-start(f32[4,128,256]{2,1,0:T(8,128)S(1)} %get-tuple-element.47), channel_id=1, source_target_pairs={{0,1},{1,0},{2,3},{3,2},{4,5},{5,4},{6,7},{7,6},{8,9},{9,8},{10,11... | collective-permute-start | bytes 1572872 | tf_op jit(solution)/shard_map/ppermute | solution.py:280
  2.6 10.4 %copy-start.5 = (bf16[256,4,128]{2,1,0:T(4,128)(2,1)S(1)}, bf16[256,4,128]{2,1,0:T(4,128)(2,1)}, u32[]{:S(2)}) copy-start(bf16[256,4,128]{2,1,0:T(4,128)(2,1)} %param.6) | copy-start | bytes 786436
  2.6 24.6 %copy-start.4 = (s32[3,512]{1,0:T(4,128)S(1)}, s32[3,512]{1,0:T(4,128)}, u32[]{:S(2)}) copy-start(s32[3,512]{1,0:T(4,128)} %cells.3) | copy-start | bytes 18436
  2.7 24.5 %collective-permute-start.2 = (f32[8,128,256]{2,1,0:T(8,128)S(1)}, f32[8,128,256]{2,1,0:T(8,128)S(1)}, u32[]{:S(2)}, u32[]{:S(2)}) collective-permute-start(f32[8,128,256]{2,1,0:T(8,128)S(1)} %pad_maximum_fusion.chip_own), channel_id=1, source_target_pairs={{1,2},{2,1},{5,6},{6,5},{9,10},{10,9},{13,14},{14,13},{17,18},{18,... | collective-permute-start | bytes 3145736 | tf_op jit(solution)/shard_map/ppermute | solution.py:281
  7.4 1.6 %copy-start.3 = (f32[1,16,128,256]{3,2,1,0:T(8,128)S(1)}, f32[1,16,128,256]{3,2,1,0:T(8,128)}, u32[]{:S(2)}) copy-start(f32[1,16,128,256]{3,2,1,0:T(8,128)} %refs_1_.1) | copy-start | bytes 6291460
  11.0 16.2 %collective-permute-start.1 = (f32[4,128,256]{2,1,0:T(8,128)S(1)}, f32[4,128,256]{2,1,0:T(8,128)S(1)}, u32[]{:S(2)}, u32[]{:S(2)}) collective-permute-start(f32[4,128,256]{2,1,0:T(8,128)S(1)} %get-tuple-element.26.first), channel_id=1, source_target_pairs={{0,1},{1,0},{2,3},{3,2},{4,5},{5,4},{6,7},{7,6},{8,9},{9,8},{10,11... | collective-permute-start | bytes 1572872 | tf_op jit(solution)/shard_map/ppermute | solution.py:280
  11.1 16.1 %collective-permute-start.3 = (f32[4,128,256]{2,1,0:T(8,128)S(1)}, f32[4,128,256]{2,1,0:T(8,128)S(1)}, u32[]{:S(2)}, u32[]{:S(2)}) collective-permute-start(f32[4,128,256]{2,1,0:T(8,128)S(1)} %get-tuple-element.24.partial), channel_id=1, source_target_pairs={{1,2},{2,1},{5,6},{6,5},{9,10},{10,9},{13,14},{14,13},{17,18},{18,... | collective-permute-start | bytes 1572872 | tf_op jit(solution)/shard_map/ppermute | solution.py:281
  30.6 3.7 %collective-permute-start.4 = (f32[4,128,256]{2,1,0:T(8,128)S(1)}, f32[4,128,256]{2,1,0:T(8,128)S(1)}, u32[]{:S(2)}, u32[]{:S(2)}) collective-permute-start(f32[4,128,256]{2,1,0:T(8,128)S(1)} %get-tuple-element.34.refs_0_.refs_3_), channel_id=1, source_target_pairs={{0,1},{1,0},{2,3},{3,2},{4,5},{5,4},{6,7},{7,6},{8,9},{9,8},{10,11... | collective-permute-start | bytes 1572872 | tf_op jit(solution)/shard_map/ppermute | solution.py:280
  31.4 10.5 %collective-permute-start.5 = (f32[4,128,256]{2,1,0:T(8,128)S(1)}, f32[4,128,256]{2,1,0:T(8,128)S(1)}, u32[]{:S(2)}, u32[]{:S(2)}) collective-permute-start(f32[4,128,256]{2,1,0:T(8,128)S(1)} %get-tuple-element.36.refs_2_.refs_5_.own), channel_id=1, source_target_pairs={{1,2},{2,1},{5,6},{6,5},{9,10},{10,9},{13,14},{14,13},{17,18},{18,... | collective-permute-start | bytes 1572872 | tf_op jit(solution)/shard_map/ppermute | solution.py:281
  37.2 6.3 %collective-permute-start.6 = (f32[4,128,256]{2,1,0:T(8,128)S(1)}, f32[4,128,256]{2,1,0:T(8,128)S(1)}, u32[]{:S(2)}, u32[]{:S(2)}) collective-permute-start(f32[4,128,256]{2,1,0:T(8,128)S(1)} %get-tuple-element.40.first.refs_0_), channel_id=1, source_target_pairs={{0,1},{1,0},{2,3},{3,2},{4,5},{5,4},{6,7},{7,6},{8,9},{9,8},{10,11... | collective-permute-start | bytes 1572872 | tf_op jit(solution)/shard_map/ppermute | solution.py:280
  37.3 10.5 %collective-permute-start.7 = (f32[4,128,256]{2,1,0:T(8,128)S(1)}, f32[4,128,256]{2,1,0:T(8,128)S(1)}, u32[]{:S(2)}, u32[]{:S(2)}) collective-permute-start(f32[4,128,256]{2,1,0:T(8,128)S(1)} %get-tuple-element.42.partial), channel_id=1, source_target_pairs={{1,2},{2,1},{5,6},{6,5},{9,10},{10,9},{13,14},{14,13},{17,18},{18,... | collective-permute-start | bytes 1572872 | tf_op jit(solution)/shard_map/ppermute | solution.py:281
